TPU v7x, 256 devices: a whole 4x4x8 slice. The times are simulated.
256 devices in a mesh: row: 8 (over y, core), col: 32 (over z, x).
Axes of the slice: x: 4, y: 4, z: 8, core: 2. Of those that a mesh axis runs over, the one named last changes fastest.
Arguments:
- residuals: bfloat16 [131072, 32], P(('row', 'col')), may hold values from -6 to 6
- intersect_blocks: int32 [256, 4], P(('row', 'col')), may hold values from 0 to 3
- local_inverse: bfloat16 [131072, 1024], P(('row', 'col')), may hold values from -0.1875 to 0.1875
- coarse_basis: float32 [262144, 64], P(('row', 'col')), may hold values from -0.1875 to 0.1875
- coarse_slots: int32 [16384], replicated, may hold values from 0 to 16383, each once
- coarse_inverse: float32 [16384, 16384], P('row', 'col'), may hold values from -0.1875 to 0.1875
Outputs:
- preconditioned: float32 [131072, 32], P(('row', 'col'))
Inputs may be any that keep to these rules, and one draw needn't show every extreme that they name: `intersect_blocks`: each entry names one of the four owned blocks. `coarse_slots`: every coarse index from 0 to 16383 appears exactly once.
All inputs are finite; a program needn't handle non-finite values.
Results may differ from a plain program's by a relative error of at most 0.0003.
Values may be sent and summed in bfloat16 or wider, within the bound.
A program may use at most 64 MiB of HBM per device.

v0:
```python
import functools

import jax
import jax.numpy as jnp
from jax import lax
from jax.experimental import pallas as pl
from jax.experimental.pallas import tpu as pltpu
from jax.sharding import PartitionSpec as P

MESH = pl.DeviceIdType.MESH
BLK = 128
LANES = 128
UNROLL = 16
FAR_NUM, FAR_DEN = 1, 2
NT = (((1,), (1,)), ((), ()))
NN = (((1,), (0,)), ((), ()))
F32 = jnp.float32
BF16 = jnp.bfloat16


def matmul(a, b, dims):
    return lax.dot_general(a, b, dims, preferred_element_type=F32)


def split(x):
    hi = x.astype(BF16)
    return hi, (x - hi.astype(F32)).astype(BF16)


def loop(start, stop, body):
    if stop - start <= UNROLL:
        for i in range(start, stop):
            body(i)
    else:
        def step(i, carry):
            body(i)
            return carry

        lax.fori_loop(start, stop, step, 0)


def flipped(index, k, count):
    out = index
    bit = 1
    while bit < count:
        kbit = (k // bit) % 2
        out = out + kbit * bit * (1 - 2 * ((index // bit) % 2))
        bit *= 2
    return out


def lane_low(shape):
    return lax.broadcasted_iota(jnp.int32, shape, len(shape) - 1) < LANES // 2


def half_roll(x):
    return pltpu.roll(x, LANES // 2, 1)


def kernel(
    nrow,
    ncol,
    res_hbm,
    ib_hbm,
    linv_hbm,
    basis_hbm,
    slots_hbm,
    coarse_hbm,
    out_ref,
    res_ref,
    ib_ref,
    slots_ref,
    outgoing,
    incoming,
    linv,
    basis,
    basis2,
    coarse,
    coarse_hi,
    coarse_lo,
    hot_in,
    hot_out,
    gathered,
    pieces,
    received,
    solved,
    lent,
    wide_hi,
    wide_lo,
    passed,
    load_sem,
    halo_send,
    halo_recv,
    lend_send,
    lend_recv,
    ag1_send,
    ag1_recv,
    ag1_rest,
    rs_send,
    rs_recv,
    ag2_send,
    ag2_recv,
    ag2_rest,
):
    r = lax.axis_index("row")
    c = lax.axis_index("col")
    me = r * ncol + c
    rhs = res_ref.shape[0]
    own = res_ref.shape[1]
    half = rhs // 2
    ndev = nrow * ncol
    rows, width = coarse.shape
    total = slots_ref.shape[1]

    near = ncol * FAR_NUM // FAR_DEN

    def col_peer(k):
        return (r, flipped(c, k, ncol))

    def row_peer(j):
        return (lax.rem(r + j, nrow), c)

    barrier = pltpu.get_barrier_semaphore()
    loop(1, ncol, lambda k: pl.semaphore_signal(barrier, inc=1, device_id=col_peer(ncol - k), device_id_type=MESH))
    loop(1, nrow, lambda j: pl.semaphore_signal(barrier, inc=1, device_id=row_peer(j), device_id_type=MESH))

    loads = [
        pltpu.make_async_copy(basis_hbm, basis, load_sem.at[0]),
        pltpu.make_async_copy(coarse_hbm, coarse, load_sem.at[1]),
        pltpu.make_async_copy(linv_hbm, linv, load_sem.at[2]),
        pltpu.make_async_copy(res_hbm, res_ref, load_sem.at[3]),
        pltpu.make_async_copy(ib_hbm, ib_ref, load_sem.at[4]),
        pltpu.make_async_copy(slots_hbm, slots_ref, load_sem.at[5]),
    ]
    for load in loads[3:] + loads[:3]:
        load.start()
    loads[4].wait()
    loads[3].wait()

    exists = [r < nrow - 1, r > 0, c < ncol - 1, c > 0]
    target = [(r + 1, c), (r - 1, c), (r, c + 1), (r, c - 1)]
    opposite = [1, 0, 3, 2]
    blocks = [res_ref[:, b * BLK:(b + 1) * BLK] for b in range(own // BLK)]
    for d in range(4):
        index = ib_ref[0, d]
        value = blocks[0]
        for b in range(1, len(blocks)):
            value = jnp.where(index == b, blocks[b], value)
        outgoing[d] = value

        @pl.when(jnp.logical_not(exists[opposite[d]]))
        def _():
            incoming[d] = jnp.zeros_like(incoming[d])

        @pl.when(jnp.logical_not(exists[d]))
        def _():
            lent[d] = jnp.zeros_like(lent[d])

    def halo(d):
        return pltpu.make_async_remote_copy(
            src_ref=outgoing.at[d], dst_ref=incoming.at[d],
            send_sem=halo_send.at[d], recv_sem=halo_recv.at[d],
            device_id=target[d], device_id_type=MESH)

    def lend(d):
        return pltpu.make_async_remote_copy(
            src_ref=basis.at[:, pl.ds(own + d * BLK, BLK)], dst_ref=lent.at[d],
            send_sem=lend_send.at[d], recv_sem=lend_recv.at[d],
            device_id=target[opposite[d]], device_id_type=MESH)

    pl.semaphore_wait(barrier, ncol + nrow - 2)
    for q in range(1, nrow // 2):
        pl.semaphore_signal(passed, inc=1, device_id=(lax.rem(r + 2 * q, nrow), c), device_id_type=MESH)
    for d in range(4):
        @pl.when(exists[d])
        def _():
            halo(d).start()

    loads[0].wait()
    nev = basis.shape[0]
    b_hi, b_lo = split(basis[...])
    basis2[:nev] = b_hi
    basis2[nev:] = b_lo
    partial = matmul(res_ref[...], basis2[:, :own], NT)

    for d in range(4):
        @pl.when(exists[opposite[d]])
        def _():
            halo(d).wait_recv()

    inc = jnp.concatenate([incoming[d] for d in range(4)], axis=1)
    partial = partial + matmul(inc, basis2[:, own:], NT)
    partial = partial + half_roll(partial)
    low = lane_low((half, LANES))
    gathered[me] = jnp.where(low, partial[:half], partial[half:])

    def spread(buf, send, recv, rest, far):
        pairs = nrow // 2
        partner = r + 1 - 2 * lax.rem(r, 2)
        singles = ncol - 1 + (pairs - 1) * (ncol - far)

        def copy(slot, sem, device):
            return pltpu.make_async_remote_copy(
                src_ref=buf.at[slot], dst_ref=buf.at[slot], send_sem=send.at[0], recv_sem=sem,
                device_id=device, device_id_type=MESH)

        def pair_row(q):
            return lax.rem(r + 2 * q, nrow)

        def start():
            def one(i):
                k = ncol - i
                for q in range(pairs if i <= ncol - far else 1):
                    copy(me, recv.at[k, q], (pair_row(q), flipped(c, k, ncol))).start()

            if far == ncol:
                loop(1, ncol, lambda i: copy(me, recv.at[ncol - i, 0], col_peer(ncol - i)).start())
            else:
                for i in range(1, ncol):
                    one(i)
            share(r * ncol + c)

        def share(slot):
            for q in range(1, pairs):
                copy(slot, rest.at[pairs - q], (pair_row(q), c)).start()
            for q in range(1, pairs):
                copy(slot, rest.at[2 * pairs - q], (lax.rem(partner + 2 * q, nrow), c)).start()
            copy(slot, rest.at[pairs], (partner, c)).start()

        def arrival(slot, k, q):
            copy(slot, recv.at[k, q], (partner, c)).wait_recv()

        def relay(first, last):
            def near(k):
                slot = r * ncol + flipped(c, k, ncol)
                arrival(slot, k, 0)
                share(slot)

            def distant(k):
                for q in range(pairs):
                    slot = pair_row(pairs - q) * ncol + flipped(c, k, ncol)
                    arrival(slot, k, q)
                    copy(slot, rest.at[pairs + (pairs - q) % pairs], (partner, c)).start()

            loop(first, min(last, far), near)
            if last > far:
                loop(max(first, far), last, distant)

        def finish(consume):
            def wait(index, count):
                some = buf.at[pl.ds(0, count)]
                pltpu.make_async_copy(some, some, rest.at[index]).wait()

            total = consume(r, None)
            wait(pairs, ncol)
            total = consume(partner, total)
            for o in range(1, pairs):
                wait(o, far)
                total = consume(pair_row(o), total)
            for o in range(1, pairs):
                wait(pairs + o, ncol)
                total = consume(lax.rem(partner + 2 * o, nrow), total)
            return total

        def drain():
            count = singles + far * (nrow - 1) + (ncol - far) * pairs
            while count > 0:
                now = min(count, ndev)
                some = buf.at[pl.ds(0, now)]
                pltpu.make_async_copy(some, some, send.at[0]).wait()
                count -= now

        return start, relay, finish, drain

    depth = ncol * nev

    def unpacked(buf, row):
        tops, bots = [], []
        for p in range(ncol // 2):
            a, b = buf[row * ncol + 2 * p], buf[row * ncol + 2 * p + 1]
            tops.append(jnp.where(low, a, half_roll(b)))
            bots.append(jnp.where(low, half_roll(a), b))
        value = jnp.concatenate([jnp.concatenate(tops, axis=1), jnp.concatenate(bots, axis=1)], axis=0)
        return jnp.concatenate(split(value), axis=0)

    def plus(total, part):
        return part if total is None else total + part

    def take_in(row, total):
        lanes = pl.ds(pl.multiple_of(row * depth, depth), depth)
        return plus(total, matmul(unpacked(gathered, row), hot_in[:, lanes], NT))

    def take_out(row, total):
        at = pl.ds(pl.multiple_of(row * depth, depth), depth)
        return plus(total, matmul(unpacked(solved, row), hot_out[at], NN))

    start1, relay1, finish1, drain1 = spread(gathered, ag1_send, ag1_recv, ag1_rest, near)
    pl.semaphore_wait(passed, nrow // 2 - 1)
    start1()

    loads[2].wait()
    local = jnp.concatenate([res_ref[...], inc], axis=1)
    out_ref[...] = matmul(local, linv[...], NT)
    relay1(1, ncol // 2)
    chunk = 2 * LANES
    loads[5].wait()

    def build_in(i):
        lanes = pl.ds(i * chunk if isinstance(i, int) else pl.multiple_of(i * chunk, chunk), chunk)
        slot = slots_ref[:, lanes] - c * width
        place = lax.broadcasted_iota(jnp.int32, (width, chunk), 0)
        hot_in[:, lanes] = jnp.where(place == slot, 1.0, 0.0).astype(BF16)

    loop(0, total // chunk, build_in)
    relay1(ncol // 2, ncol)
    loads[1].wait()
    a_hi, a_lo = split(coarse[...])
    coarse_hi[...] = a_hi
    coarse_lo[...] = a_lo
    column = finish1(take_in)
    for d in range(4):
        @pl.when(exists[opposite[d]])
        def _():
            lend(d).start()

    column_hi, column_lo = split(column[:rhs] + column[rhs:])
    column2 = jnp.concatenate([column_hi, column_lo], axis=0)
    span = 2 * LANES

    def reduce(peer):
        return pltpu.make_async_remote_copy(
            src_ref=pieces.at[peer], dst_ref=received.at[c],
            send_sem=rs_send.at[0], recv_sem=rs_recv.at[0],
            device_id=(r, peer), device_id_type=MESH)

    group = 2 * (span // LANES)

    def product(i):
        block = lax.rem(c // group + 1 + i, rows // span)
        at = pl.ds(pl.multiple_of(block * span, span), span)
        part = matmul(column2, coarse_hi[at], NT) + matmul(column2, coarse_lo[at], NT)
        part = part[:rhs] + part[rhs:]
        for q in range(span // LANES):
            top = part[:half, q * LANES:(q + 1) * LANES]
            bot = part[half:, q * LANES:(q + 1) * LANES]
            pieces[block * group + 2 * q] = jnp.where(low, top, half_roll(bot))
            pieces[block * group + 2 * q + 1] = jnp.where(low, half_roll(top), bot)

        for q in range(group):
            @pl.when(block * group + q != c)
            def _():
                reduce(block * group + q).start()

    loop(0, rows // span, product)

    low8 = lane_low((8, LANES))

    def slots_of(device):
        device = jnp.clip(device, 0, ndev - 1)
        at = pl.ds(pl.multiple_of((device // 2) * LANES, LANES), LANES)
        pair = jnp.broadcast_to(slots_ref[:, at], (8, LANES))
        swapped = half_roll(pair)
        return jnp.where(lax.rem(device, 2) == 0, jnp.where(low8, pair, swapped), jnp.where(low8, swapped, pair))

    mine = [
        jnp.where(low8, slots_of(me), slots_of(me + ncol))[:1],
        jnp.where(low8, slots_of(me - ncol), slots_of(me + 1))[:1],
        jnp.where(low8, slots_of(me - 1), -1)[:1],
    ]
    tall = 4 * LANES

    def build_out(i):
        at = pl.ds(i * tall if isinstance(i, int) else pl.multiple_of(i * tall, tall), tall)
        place = lax.broadcasted_iota(jnp.int32, (tall, LANES), 0) + i * tall
        for q in range(3):
            hot_out[at, q * LANES:(q + 1) * LANES] = jnp.where(place == mine[q], 1.0, 0.0).astype(BF16)

    loop(0, total // tall, build_out)

    wide_hi[:nev] = basis2[:nev, :own]
    wide_lo[:nev] = basis2[nev:, :own]
    wide_hi[5 * nev:] = jnp.zeros_like(wide_hi[5 * nev:])
    wide_lo[5 * nev:] = jnp.zeros_like(wide_lo[5 * nev:])
    for d in range(4):
        @pl.when(exists[d])
        def _():
            lend(d).wait_recv()

        l_hi, l_lo = split(lent[d])
        for b in range(own // BLK):
            here = ib_ref[0, d] == b
            at = slice((d + 1) * nev, (d + 2) * nev), slice(b * BLK, (b + 1) * BLK)
            wide_hi[at] = jnp.where(here, l_hi, jnp.zeros_like(l_hi))
            wide_lo[at] = jnp.where(here, l_lo, jnp.zeros_like(l_lo))

    others = received.at[pl.ds(0, ncol - 1)]
    pltpu.make_async_copy(others, others, rs_recv.at[0]).wait()
    summed = pieces[c]
    if ncol - 1 <= UNROLL:
        for k in range(1, ncol):
            summed = summed + received[flipped(c, k, ncol)]
    else:
        summed = lax.fori_loop(1, ncol, lambda k, acc: acc + received[flipped(c, k, ncol)], summed)
    solved[me] = summed

    start2, relay2, finish2, drain2 = spread(solved, ag2_send, ag2_recv, ag2_rest, near)
    start2()
    relay2(1, ncol)
    picked = finish2(take_out)
    picked = picked.astype(BF16)

    inner = matmul(picked, wide_hi[...], NN) + matmul(picked, wide_lo[...], NN)
    out_ref[...] = out_ref[...] + inner[:rhs] + inner[rhs:]

    drain1()
    drain2()
    pltpu.make_async_copy(others, others, rs_send.at[0]).wait()
    for d in range(4):
        @pl.when(exists[d])
        def _():
            halo(d).wait_send()

        @pl.when(exists[opposite[d]])
        def _():
            lend(d).wait_send()


def shards(nrow, ncol, residuals, intersect_blocks, local_inverse, coarse_basis, coarse_slots, coarse_inverse):
    own, rhs = residuals.shape
    loc, nev = coarse_basis.shape
    rows, width = coarse_inverse.shape
    total = coarse_slots.shape[0]
    ndev = nrow * ncol
    assert 2 * nev == LANES and rows == ncol * nev and loc == own + 4 * BLK and own % BLK == 0
    packed = (rhs // 2, LANES)
    vmem = pl.BlockSpec(memory_space=pltpu.VMEM)
    hbm = pl.BlockSpec(memory_space=pl.ANY)
    dma = pltpu.SemaphoreType.DMA
    out = pl.pallas_call(
        functools.partial(kernel, nrow, ncol),
        name="schwarz",
        out_shape=pltpu.VMEM((rhs, own), F32),
        in_specs=[hbm] * 6,
        out_specs=vmem,
        scratch_shapes=[
            pltpu.VMEM((rhs, own), BF16),
            pltpu.SMEM(intersect_blocks.shape, jnp.int32),
            pltpu.VMEM((1, total), jnp.int32),
            pltpu.VMEM((4, rhs, BLK), BF16),
            pltpu.VMEM((4, rhs, BLK), BF16),
            pltpu.VMEM((own, loc), BF16),
            pltpu.VMEM((nev, loc), F32),
            pltpu.VMEM((2 * nev, loc), BF16),
            pltpu.VMEM((rows, width), F32),
            pltpu.VMEM((rows, width), BF16),
            pltpu.VMEM((rows, width), BF16),
            pltpu.VMEM((width, total), BF16),
            pltpu.VMEM((total, 3 * LANES), BF16),
            pltpu.VMEM((ndev,) + packed, F32),
            pltpu.VMEM((ncol,) + packed, F32),
            pltpu.VMEM((ncol,) + packed, F32),
            pltpu.VMEM((ndev,) + packed, F32),
            pltpu.VMEM((4, nev, BLK), F32),
            pltpu.VMEM((6 * nev, own), BF16),
            pltpu.VMEM((6 * nev, own), BF16),
            pltpu.SemaphoreType.REGULAR,
            dma((6,)),
            dma((4,)),
            dma((4,)),
            dma((4,)),
            dma((4,)),
            dma((1,)),
            dma((ncol, nrow // 2)),
            dma((nrow,)),
            dma((1,)),
            dma((1,)),
            dma((1,)),
            dma((ncol, nrow // 2)),
            dma((nrow,)),
        ],
        compiler_params=pltpu.CompilerParams(collective_id=0, has_side_effects=True),
    )(
        residuals.T,
        intersect_blocks,
        local_inverse,
        coarse_basis.T,
        coarse_slots.reshape(1, total),
        coarse_inverse,
    )
    return out.T


def solution(mesh):
    placed = (
        P(("row", "col"), None),
        P(("row", "col"), None),
        P(("row", "col"), None),
        P(("row", "col"), None),
        P(),
        P("row", "col"),
    )
    return jax.shard_map(
        functools.partial(shards, mesh.shape["row"], mesh.shape["col"]),
        mesh=mesh, in_specs=placed, out_specs=P(("row", "col"), None), check_vma=False,
    )
```

profile of v0, /device:TPU:1, one launch (start us, length us, event | category | flops | bytes accessed | tf_op | source)
XLA Modules:
  0.0 92.1 jit_solution(17505540257938386911)
XLA Ops:
  0.0 91.5 %schwarz.1 = f32[32,512]{1,0:T(8,128)S(1)} custom-call(bf16[32,512]{1,0:T(8,128)(2,1)} %bitcast.7, s32[1,4]{1,0:T(1,128)} %ib_hbm.1, bf16[512,1024]{1,0:T(8,128)(2,1)} %linv_hbm.1, f32[64,1024]{1,0:T(8,128)} %bitcast.5, s32[1,16384]{1,0:T(1,128)} %bitcast.6, f32[2048,512]{1,0:T(8,128)} %coarse_hbm.1), custom_call_target="tpu_custom_call" | custom-call | tf_op jit(solution)/shard_map/schwarz/pallas_call | solution.py:439
  91.5 0.6 copy.8
where the time goes:
time: 93.1 us; the launch traced here: 92.1 us
  Pallas kernels  91.5 us (98%)
    pallas_call x1, Pallas kernels, shards(): pl.pallas_call(functools.partial(kernel, nrow, ncol), name='schwarz', out...  91.5 us

commit v1 on v0

v1 whole, which is shorter than its diff:
```python
import functools

import jax
import jax.numpy as jnp
from jax import lax
from jax.experimental import pallas as pl
from jax.experimental.pallas import tpu as pltpu
from jax.sharding import PartitionSpec as P

MESH = pl.DeviceIdType.MESH
BLK = 128
LANES = 128
NX = 4
CORES = 2
NT = (((1,), (1,)), ((), ()))
NN = (((1,), (0,)), ((), ()))
F32 = jnp.float32
BF16 = jnp.bfloat16


def matmul(a, b, dims):
    return lax.dot_general(a, b, dims, preferred_element_type=F32)


def split(x):
    hi = x.astype(BF16)
    return hi, (x - hi.astype(F32)).astype(BF16)


def lane_low(shape):
    return lax.broadcasted_iota(jnp.int32, shape, len(shape) - 1) < LANES // 2


def half_roll(x):
    return pltpu.roll(x, LANES // 2, 1)


def far_first(count):
    return sorted(range(1, count), key=lambda k: -min(k, count - k))


def tree_sum(parts):
    while len(parts) > 1:
        parts = [parts[i] + parts[i + 1] if i + 1 < len(parts) else parts[i] for i in range(0, len(parts), 2)]
    return parts[0]


def kernel(
    nrow,
    ncol,
    res_hbm,
    ib_hbm,
    linv_hbm,
    basis_hbm,
    slots_hbm,
    coarse_hbm,
    out_ref,
    res_ref,
    ib_ref,
    slots_ref,
    outgoing,
    incoming,
    linv,
    basis,
    basis2,
    coarse,
    coarse_hi,
    coarse_lo,
    hot_in,
    hot_out,
    plane1,
    cross1,
    line1,
    rhs_all,
    pieces,
    received,
    plane2,
    cross2,
    line2,
    picks,
    lent,
    wide_hi,
    wide_lo,
    load_sem,
    halo_send,
    halo_recv,
    lend_send,
    lend_recv,
    pick_send,
    pick_recv,
    bulk_send,
    bulk_recv,
):
    r = lax.axis_index("row")
    c = lax.axis_index("col")
    z, x = c // NX, lax.rem(c, NX)
    y, core = r // CORES, lax.rem(r, CORES)
    nz, ny = ncol // NX, nrow // CORES
    nplane = nrow * NX
    rhs = res_ref.shape[0]
    own = res_ref.shape[1]
    half = rhs // 2
    rows, width = coarse.shape
    nev = basis.shape[0]
    low = lane_low((half, LANES))
    mine = r * NX + x

    def row_at(dy, dk):
        return lax.rem(y + dy, ny) * CORES + lax.rem(core + dk, CORES)

    plane_offsets = sorted(
        ((dx, dy, dk) for dx in range(NX) for dy in range(ny) for dk in range(CORES) if (dx, dy, dk) != (0, 0, 0)),
        key=lambda o: -(min(o[0], NX - o[0]) + min(o[1], ny - o[1]) + 0.5 * o[2]))
    row_offsets = [(dy, dk) for dx, dy, dk in plane_offsets if dx == 0]

    def plane_peer(dx, dy, dk):
        return (row_at(dy, dk), z * NX + lax.rem(x + dx, NX))

    def line_peer(dz):
        return (r, lax.rem(z + dz, nz) * NX + x)

    exists = [r < nrow - 1, r > 0, c < ncol - 1, c > 0]
    target = [(r + 1, c), (r - 1, c), (r, c + 1), (r, c - 1)]
    opposite = [1, 0, 3, 2]
    up = jnp.logical_and(x == NX - 1, exists[2])
    down = jnp.logical_and(x == 0, exists[3])

    barrier = pltpu.get_barrier_semaphore()

    def greet(device):
        pl.semaphore_signal(barrier, inc=1, device_id=device, device_id_type=MESH)

    for offset in plane_offsets:
        greet(plane_peer(*offset))
    for dz in far_first(nz):
        greet(line_peer(dz))

    @pl.when(up)
    def _():
        greet(target[2])

    @pl.when(down)
    def _():
        greet(target[3])

    loads = [
        pltpu.make_async_copy(basis_hbm, basis, load_sem.at[0]),
        pltpu.make_async_copy(coarse_hbm, coarse, load_sem.at[1]),
        pltpu.make_async_copy(linv_hbm, linv, load_sem.at[2]),
        pltpu.make_async_copy(res_hbm, res_ref, load_sem.at[3]),
        pltpu.make_async_copy(ib_hbm, ib_ref, load_sem.at[4]),
        pltpu.make_async_copy(slots_hbm, slots_ref, load_sem.at[5]),
    ]
    for i in (3, 4, 0, 5, 1, 2):
        loads[i].start()
    loads[4].wait()
    loads[3].wait()

    blocks = [res_ref[:, b * BLK:(b + 1) * BLK] for b in range(own // BLK)]
    for d in range(4):
        index = ib_ref[0, d]
        value = blocks[0]
        for b in range(1, len(blocks)):
            value = jnp.where(index == b, blocks[b], value)
        outgoing[d] = value

        @pl.when(jnp.logical_not(exists[opposite[d]]))
        def _():
            incoming[d] = jnp.zeros_like(incoming[d])

        @pl.when(jnp.logical_not(exists[d]))
        def _():
            lent[d] = jnp.zeros_like(lent[d])
            picks[1 + d] = jnp.zeros_like(picks[1 + d])

    picks[5] = jnp.zeros_like(picks[5])

    def halo(d):
        return pltpu.make_async_remote_copy(
            src_ref=outgoing.at[d], dst_ref=incoming.at[d],
            send_sem=halo_send.at[d], recv_sem=halo_recv.at[d],
            device_id=target[d], device_id_type=MESH)

    def lend(d):
        return pltpu.make_async_remote_copy(
            src_ref=basis.at[:, pl.ds(own + d * BLK, BLK)], dst_ref=lent.at[d],
            send_sem=lend_send.at[d], recv_sem=lend_recv.at[d],
            device_id=target[opposite[d]], device_id_type=MESH)

    def pick(d):
        return pltpu.make_async_remote_copy(
            src_ref=picks.at[0], dst_ref=picks.at[1 + d],
            send_sem=pick_send.at[d], recv_sem=pick_recv.at[d],
            device_id=target[opposite[d]], device_id_type=MESH)

    def send(phase, src, dst, device):
        pltpu.make_async_remote_copy(
            src_ref=src, dst_ref=dst, send_sem=bulk_send.at[phase], recv_sem=bulk_recv.at[phase],
            device_id=device, device_id_type=MESH).start()

    def arrived(phase, buf, count):
        some = buf.at[pl.ds(0, count)]
        pltpu.make_async_copy(some, some, bulk_recv.at[phase]).wait()

    def drained(phase, buf, count):
        some = buf.at[pl.ds(0, count)]
        pltpu.make_async_copy(some, some, bulk_send.at[phase]).wait()

    def spread_plane(phase, buf):
        for offset in plane_offsets:
            send(phase, buf.at[mine], buf.at[mine], plane_peer(*offset))

    def exchange_line(phase, src, dst):
        for dz in far_first(nz):
            to = lax.rem(z + dz, nz)
            send(phase, src.at[to], dst.at[z], (r, to * NX + x))

    def unpacked(buf, count):
        tops, bots = [], []
        for p in range(count // 2):
            a, b = buf[2 * p], buf[2 * p + 1]
            tops.append(jnp.where(low, a, half_roll(b)))
            bots.append(jnp.where(low, half_roll(a), b))
        value = jnp.concatenate([jnp.concatenate(tops, axis=1), jnp.concatenate(bots, axis=1)], axis=0)
        return jnp.concatenate(split(value), axis=0)

    def packed(part, put):
        for q in range(part.shape[1] // LANES):
            top = part[:half, q * LANES:(q + 1) * LANES]
            bot = part[half:, q * LANES:(q + 1) * LANES]
            put(2 * q, jnp.where(low, top, half_roll(bot)))
            put(2 * q + 1, jnp.where(low, half_roll(top), bot))

    plane_width = NX * nev
    share = width // nrow
    loads[5].wait()
    place_in = lax.broadcasted_iota(jnp.int32, (share, plane_width), 0)

    def build_in(i, carry):
        start = pl.multiple_of(i * (ncol * nev) + z * plane_width, plane_width)
        slot = slots_ref[:, pl.ds(start, plane_width)] - (x * width + r * share)
        at = pl.ds(pl.multiple_of(i * plane_width, plane_width), plane_width)
        for t in range(nz):
            hot = jnp.where(place_in == slot - t * (NX * width), 1.0, 0.0)
            hot_in[t * share:(t + 1) * share, at] = hot.astype(BF16)
        return carry

    lax.fori_loop(0, nrow, build_in, 0)

    loads[0].wait()
    b_hi, b_lo = split(basis[...])
    basis2[:nev] = b_hi
    basis2[nev:] = b_lo
    partial = matmul(res_ref[...], basis2[:, :own], NT)

    extra = up.astype(jnp.int32) + down.astype(jnp.int32)
    pl.semaphore_wait(barrier, nplane - 1 + nz - 1 + extra)
    for d in range(4):
        @pl.when(exists[d])
        def _():
            halo(d).start()
    for d in range(4):
        @pl.when(exists[opposite[d]])
        def _():
            lend(d).start()

    loads[1].wait()
    a_hi, a_lo = split(coarse[...])
    coarse_hi[...] = a_hi
    coarse_lo[...] = a_lo

    for d in range(4):
        @pl.when(exists[opposite[d]])
        def _():
            halo(d).wait_recv()

    inc = jnp.concatenate([incoming[d] for d in range(4)], axis=1)
    partial = partial + matmul(inc, basis2[:, own:], NT)
    partial = partial + half_roll(partial)
    plane1[mine] = jnp.where(low, partial[:half], partial[half:])
    spread_plane(0, plane1)

    loads[2].wait()
    local = jnp.concatenate([res_ref[...], inc], axis=1)
    out_ref[...] = matmul(local, linv[...], NT)

    low8 = lane_low((8, LANES))
    wanted = []
    for t in range(nz // 2):
        pair = []
        for device in (r * ncol + 2 * t * NX + x, r * ncol + (2 * t + 1) * NX + x):
            at = pl.ds(pl.multiple_of((device // 2) * LANES, LANES), LANES)
            pair.append(jnp.broadcast_to(slots_ref[:, at], (8, LANES)))
        even = jnp.where(low8, pair[0], half_roll(pair[1]))
        odd = jnp.where(low8, half_roll(pair[0]), pair[1])
        wanted.append(jnp.where(lax.rem(x, 2) == 0, even, odd)[:1])
    wanted = jnp.concatenate(wanted, axis=1)
    place_out = lax.broadcasted_iota(jnp.int32, (plane_width, nz * nev), 0)

    def build_out(i, carry):
        at = pl.ds(pl.multiple_of(i * plane_width, plane_width), plane_width)
        hot = jnp.where(place_out == wanted - (i * rows + z * plane_width), 1.0, 0.0)
        hot_out[at] = hot.astype(BF16)
        return carry

    lax.fori_loop(0, nrow, build_out, 0)

    wide_hi[:nev] = basis2[:nev, :own]
    wide_lo[:nev] = basis2[nev:, :own]
    wide_hi[5 * nev:] = jnp.zeros_like(wide_hi[5 * nev:])
    wide_lo[5 * nev:] = jnp.zeros_like(wide_lo[5 * nev:])
    for d in range(4):
        @pl.when(exists[d])
        def _():
            lend(d).wait_recv()

        l_hi, l_lo = split(lent[d])
        for b in range(own // BLK):
            here = ib_ref[0, d] == b
            at = slice((d + 1) * nev, (d + 2) * nev), slice(b * BLK, (b + 1) * BLK)
            wide_hi[at] = jnp.where(here, l_hi, jnp.zeros_like(l_hi))
            wide_lo[at] = jnp.where(here, l_lo, jnp.zeros_like(l_lo))

    def select(phase, plane, hot, dims, cross, line):
        arrived(phase, plane, nplane - 1)
        part = matmul(unpacked(plane, nplane), hot[...], dims)
        part = part[:rhs] + part[rhs:]

        def put(i, value):
            cross[i] = value

        packed(part, put)
        exchange_line(phase + 1, cross, line)
        line[z] = cross[z]
        arrived(phase + 1, line, nz - 1)
        return tree_sum([line[i] for i in range(nz)])

    rhs_all[r] = select(0, plane1, hot_in, NT, cross1, line1)
    for dy, dk in row_offsets:
        send(2, rhs_all.at[r], rhs_all.at[r], (row_at(dy, dk), c))
    arrived(2, rhs_all, nrow - 1)
    column2 = unpacked(rhs_all, nrow)

    span = rows // nz
    for dz in far_first(nz) + [0]:
        block = lax.rem(z + dz, nz)
        at = pl.ds(pl.multiple_of(block * span, span), span)
        part = matmul(column2, coarse_hi[at], NT) + matmul(column2, coarse_lo[at], NT)

        def put(i, value):
            pieces[block * NX + i] = value

        packed(part[:rhs] + part[rhs:], put)
        for dx in (2, 1, 3, 0) if dz else (2, 1, 3):
            to = block * NX + lax.rem(x + dx, NX)
            send(3, pieces.at[to], received.at[c], (r, to))

    received[c] = pieces[c]
    arrived(3, received, ncol - 1)
    plane2[mine] = tree_sum([received[i] for i in range(ncol)])

    spread_plane(4, plane2)
    picks[0] = select(4, plane2, hot_out, NN, cross2, line2)
    for d in range(4):
        @pl.when(exists[opposite[d]])
        def _():
            pick(d).start()
    for d in range(4):
        @pl.when(exists[d])
        def _():
            pick(d).wait_recv()

    picked = unpacked(picks, 6)
    inner = matmul(picked, wide_hi[...], NN) + matmul(picked, wide_lo[...], NN)
    out_ref[...] = out_ref[...] + inner[:rhs] + inner[rhs:]

    drained(0, plane1, nplane - 1)
    drained(1, line1, nz - 1)
    drained(2, rhs_all, nrow - 1)
    drained(3, received, ncol - 1)
    drained(4, plane2, nplane - 1)
    drained(5, line2, nz - 1)
    for d in range(4):
        @pl.when(exists[d])
        def _():
            halo(d).wait_send()

        @pl.when(exists[opposite[d]])
        def _():
            lend(d).wait_send()
            pick(d).wait_send()


def shards(nrow, ncol, residuals, intersect_blocks, local_inverse, coarse_basis, coarse_slots, coarse_inverse):
    own, rhs = residuals.shape
    loc, nev = coarse_basis.shape
    rows, width = coarse_inverse.shape
    total = coarse_slots.shape[0]
    nz = ncol // NX
    nplane = nrow * NX
    assert 2 * nev == LANES and rows == ncol * nev and width == nrow * nev and loc == own + 4 * BLK and own % BLK == 0
    packed = (rhs // 2, LANES)
    vmem = pl.BlockSpec(memory_space=pltpu.VMEM)
    hbm = pl.BlockSpec(memory_space=pl.ANY)
    dma = pltpu.SemaphoreType.DMA
    out = pl.pallas_call(
        functools.partial(kernel, nrow, ncol),
        name="schwarz",
        out_shape=pltpu.VMEM((rhs, own), F32),
        in_specs=[hbm] * 6,
        out_specs=vmem,
        scratch_shapes=[
            pltpu.VMEM((rhs, own), BF16),
            pltpu.SMEM(intersect_blocks.shape, jnp.int32),
            pltpu.VMEM((1, total), jnp.int32),
            pltpu.VMEM((4, rhs, BLK), BF16),
            pltpu.VMEM((4, rhs, BLK), BF16),
            pltpu.VMEM((own, loc), BF16),
            pltpu.VMEM((nev, loc), F32),
            pltpu.VMEM((2 * nev, loc), BF16),
            pltpu.VMEM((rows, width), F32),
            pltpu.VMEM((rows, width), BF16),
            pltpu.VMEM((rows, width), BF16),
            pltpu.VMEM((nz * nev, nplane * nev), BF16),
            pltpu.VMEM((nplane * nev, nz * nev), BF16),
            pltpu.VMEM((nplane,) + packed, F32),
            pltpu.VMEM((nz,) + packed, F32),
            pltpu.VMEM((nz,) + packed, F32),
            pltpu.VMEM((nrow,) + packed, F32),
            pltpu.VMEM((ncol,) + packed, F32),
            pltpu.VMEM((ncol,) + packed, F32),
            pltpu.VMEM((nplane,) + packed, F32),
            pltpu.VMEM((nz,) + packed, F32),
            pltpu.VMEM((nz,) + packed, F32),
            pltpu.VMEM((6,) + packed, F32),
            pltpu.VMEM((4, nev, BLK), F32),
            pltpu.VMEM((6 * nev, own), BF16),
            pltpu.VMEM((6 * nev, own), BF16),
            dma((6,)),
            dma((4,)),
            dma((4,)),
            dma((4,)),
            dma((4,)),
            dma((4,)),
            dma((4,)),
            dma((6,)),
            dma((6,)),
        ],
        compiler_params=pltpu.CompilerParams(collective_id=0, has_side_effects=True),
    )(
        residuals.T,
        intersect_blocks,
        local_inverse,
        coarse_basis.T,
        coarse_slots.reshape(1, total),
        coarse_inverse,
    )
    return out.T


def solution(mesh):
    placed = (
        P(("row", "col"), None),
        P(("row", "col"), None),
        P(("row", "col"), None),
        P(("row", "col"), None),
        P(),
        P("row", "col"),
    )
    return jax.shard_map(
        functools.partial(shards, mesh.shape["row"], mesh.shape["col"]),
        mesh=mesh, in_specs=placed, out_specs=P(("row", "col"), None), check_vma=False,
    )
```

time: 93.1 us -> 52.9 us (0.57); the launches traced: 92.1 us -> 52.8 us
  Pallas kernels: 91.5 us -> 52.2 us
    pallas_call x1, Pallas kernels: 91.5 us -> 52.2 us  [shards(): pl.pallas_call(functools.partial(kernel, nrow, ncol), name='schwarz', out...]
where the time goes in v1:
time: 52.9 us; the launch traced here: 52.8 us
  Pallas kernels  52.2 us (99%)
  local copies, waits for them, and re-layouts  0.63 us (1%)
    pallas_call x1, Pallas kernels, shards(): pl.pallas_call(functools.partial(kernel, nrow, ncol), name='schwarz', out...  52.2 us

profile of v1, /device:TPU:1, one launch (start us, length us, event | category | flops | bytes accessed | tf_op | source)
XLA Modules:
  0.0 52.8 jit_solution(18327415931087055472)
XLA Ops:
  0.0 52.2 %schwarz.1 = f32[32,512]{1,0:T(8,128)S(1)} custom-call(bf16[32,512]{1,0:T(8,128)(2,1)} %bitcast.7, s32[1,4]{1,0:T(1,128)} %ib_hbm.1, bf16[512,1024]{1,0:T(8,128)(2,1)} %linv_hbm.1, f32[64,1024]{1,0:T(8,128)} %bitcast.5, s32[1,16384]{1,0:T(1,128)} %bitcast.6, f32[2048,512]{1,0:T(8,128)} %coarse_hbm.1), custom_call_target="tpu_custom_call" | custom-call | tf_op jit(solution)/shard_map/schwarz/pallas_call | solution.py:406
  52.2 0.6 %copy.8 = f32[512,32]{0,1:T(8,128)} copy(f32[512,32]{0,1:T(8,128)S(1)} %bitcast.4) | data formatting | bytes 131072

commit v2 on v1

--- a/solution.py
+++ b/solution.py
@@ -64,8 +64,7 @@
     basis,
     basis2,
     coarse,
-    coarse_hi,
-    coarse_lo,
+    coarse_t,
     hot_in,
     hot_out,
     plane1,
@@ -231,6 +230,13 @@
             put(2 * q, jnp.where(low, top, half_roll(bot)))
             put(2 * q + 1, jnp.where(low, half_roll(top), bot))
 
+    extra = up.astype(jnp.int32) + down.astype(jnp.int32)
+    pl.semaphore_wait(barrier, nplane - 1 + nz - 1 + extra)
+    for d in range(4):
+        @pl.when(exists[d])
+        def _():
+            halo(d).start()
+
     plane_width = NX * nev
     share = width // nrow
     loads[5].wait()
@@ -253,22 +259,6 @@
     basis2[nev:] = b_lo
     partial = matmul(res_ref[...], basis2[:, :own], NT)
 
-    extra = up.astype(jnp.int32) + down.astype(jnp.int32)
-    pl.semaphore_wait(barrier, nplane - 1 + nz - 1 + extra)
-    for d in range(4):
-        @pl.when(exists[d])
-        def _():
-            halo(d).start()
-    for d in range(4):
-        @pl.when(exists[opposite[d]])
-        def _():
-            lend(d).start()
-
-    loads[1].wait()
-    a_hi, a_lo = split(coarse[...])
-    coarse_hi[...] = a_hi
-    coarse_lo[...] = a_lo
-
     for d in range(4):
         @pl.when(exists[opposite[d]])
         def _():
@@ -279,6 +269,12 @@
     partial = partial + half_roll(partial)
     plane1[mine] = jnp.where(low, partial[:half], partial[half:])
     spread_plane(0, plane1)
+
+    span = rows // nz
+    loads[1].wait()
+    for t in range(nz):
+        at = slice(t * span, (t + 1) * span)
+        coarse_t[:width, at], coarse_t[width:, at] = split(coarse[at].T)
 
     loads[2].wait()
     local = jnp.concatenate([res_ref[...], inc], axis=1)
@@ -305,6 +301,51 @@
 
     lax.fori_loop(0, nrow, build_out, 0)
 
+    def select(phase, plane, hot, dims, cross, line, meanwhile):
+        arrived(phase, plane, nplane - 1)
+        part = matmul(unpacked(plane, nplane), hot[...], dims)
+        part = part[:rhs] + part[rhs:]
+
+        def put(i, value):
+            cross[i] = value
+
+        packed(part, put)
+        exchange_line(phase + 1, cross, line)
+        line[z] = cross[z]
+        meanwhile()
+        arrived(phase + 1, line, nz - 1)
+        return tree_sum([line[i] for i in range(nz)])
+
+    def lend_all():
+        for d in range(4):
+            @pl.when(exists[opposite[d]])
+            def _():
+                lend(d).start()
+
+    rhs_all[r] = select(0, plane1, hot_in, NT, cross1, line1, lend_all)
+    for dy, dk in row_offsets:
+        send(2, rhs_all.at[r], rhs_all.at[r], (row_at(dy, dk), c))
+    arrived(2, rhs_all, nrow - 1)
+    column2 = unpacked(rhs_all, nrow)
+
+    column4 = jnp.concatenate([column2, column2], axis=1)
+    steps = far_first(nz) + [0]
+    for batch in (steps[:nz // 2], steps[nz // 2:]):
+        parts = []
+        for dz in batch:
+            block = lax.rem(z + dz, nz)
+            at = pl.ds(pl.multiple_of(block * span, span), span)
+            parts.append((block, matmul(column4, coarse_t[:, at], NN)))
+        for block, part in parts:
+            def put(i, value):
+                pieces[block * NX + i] = value
+
+            packed(part[:rhs] + part[rhs:], put)
+        for dz, (block, part) in zip(batch, parts):
+            for dx in (2, 1, 3, 0) if dz else (2, 1, 3):
+                to = block * NX + lax.rem(x + dx, NX)
+                send(3, pieces.at[to], received.at[c], (r, to))
+
     wide_hi[:nev] = basis2[:nev, :own]
     wide_lo[:nev] = basis2[nev:, :own]
     wide_hi[5 * nev:] = jnp.zeros_like(wide_hi[5 * nev:])
@@ -321,46 +362,12 @@
             wide_hi[at] = jnp.where(here, l_hi, jnp.zeros_like(l_hi))
             wide_lo[at] = jnp.where(here, l_lo, jnp.zeros_like(l_lo))
 
-    def select(phase, plane, hot, dims, cross, line):
-        arrived(phase, plane, nplane - 1)
-        part = matmul(unpacked(plane, nplane), hot[...], dims)
-        part = part[:rhs] + part[rhs:]
-
-        def put(i, value):
-            cross[i] = value
-
-        packed(part, put)
-        exchange_line(phase + 1, cross, line)
-        line[z] = cross[z]
-        arrived(phase + 1, line, nz - 1)
-        return tree_sum([line[i] for i in range(nz)])
-
-    rhs_all[r] = select(0, plane1, hot_in, NT, cross1, line1)
-    for dy, dk in row_offsets:
-        send(2, rhs_all.at[r], rhs_all.at[r], (row_at(dy, dk), c))
-    arrived(2, rhs_all, nrow - 1)
-    column2 = unpacked(rhs_all, nrow)
-
-    span = rows // nz
-    for dz in far_first(nz) + [0]:
-        block = lax.rem(z + dz, nz)
-        at = pl.ds(pl.multiple_of(block * span, span), span)
-        part = matmul(column2, coarse_hi[at], NT) + matmul(column2, coarse_lo[at], NT)
-
-        def put(i, value):
-            pieces[block * NX + i] = value
-
-        packed(part[:rhs] + part[rhs:], put)
-        for dx in (2, 1, 3, 0) if dz else (2, 1, 3):
-            to = block * NX + lax.rem(x + dx, NX)
-            send(3, pieces.at[to], received.at[c], (r, to))
-
     received[c] = pieces[c]
     arrived(3, received, ncol - 1)
     plane2[mine] = tree_sum([received[i] for i in range(ncol)])
 
     spread_plane(4, plane2)
-    picks[0] = select(4, plane2, hot_out, NN, cross2, line2)
+    picks[0] = select(4, plane2, hot_out, NN, cross2, line2, lambda: None)
     for d in range(4):
         @pl.when(exists[opposite[d]])
         def _():
@@ -419,8 +426,7 @@
             pltpu.VMEM((nev, loc), F32),
             pltpu.VMEM((2 * nev, loc), BF16),
             pltpu.VMEM((rows, width), F32),
-            pltpu.VMEM((rows, width), BF16),
-            pltpu.VMEM((rows, width), BF16),
+            pltpu.VMEM((2 * width, rows), BF16),
             pltpu.VMEM((nz * nev, nplane * nev), BF16),
             pltpu.VMEM((nplane * nev, nz * nev), BF16),
             pltpu.VMEM((nplane,) + packed, F32),

time: 52.9 us -> 52.7 us (level)
  no operation moved by 1% of the time
where the time goes in v2:
time: 52.7 us; the launch traced here: 52.6 us
  Pallas kernels  52 us (99%)
  local copies, waits for them, and re-layouts  0.63 us (1%)
    pallas_call x1, Pallas kernels, shards(): pl.pallas_call(functools.partial(kernel, nrow, ncol), name='schwarz', out...  52 us

profile of v2, /device:TPU:1, one launch (start us, length us, event | category | flops | bytes accessed | tf_op | source)
XLA Modules:
  0.0 52.6 jit_solution(12982838669900743387)
XLA Ops:
  0.0 52.0 %schwarz.1 = f32[32,512]{1,0:T(8,128)S(1)} custom-call(bf16[32,512]{1,0:T(8,128)(2,1)} %bitcast.7, s32[1,4]{1,0:T(1,128)} %ib_hbm.1, bf16[512,1024]{1,0:T(8,128)(2,1)} %linv_hbm.1, f32[64,1024]{1,0:T(8,128)} %bitcast.5, s32[1,16384]{1,0:T(1,128)} %bitcast.6, f32[2048,512]{1,0:T(8,128)} %coarse_hbm.1), custom_call_target="tpu_custom_call" | custom-call | tf_op jit(solution)/shard_map/schwarz/pallas_call | solution.py:413
  52.0 0.6 %copy.8 = f32[512,32]{0,1:T(8,128)} copy(f32[512,32]{0,1:T(8,128)S(1)} %bitcast.4) | data formatting | bytes 131072

commit v3 on v2

v3 whole, which is shorter than its diff:
```python
import functools

import jax
import jax.numpy as jnp
from jax import lax
from jax.experimental import pallas as pl
from jax.experimental.pallas import tpu as pltpu
from jax.sharding import PartitionSpec as P

MESH = pl.DeviceIdType.MESH
BLK = 128
LANES = 128
NX = 4
CORES = 2
PEAK = 32760.0
STEPS = 8.0
TINY = 1e-30
NT = (((1,), (1,)), ((), ()))
NN = (((1,), (0,)), ((), ()))
F32 = jnp.float32
BF16 = jnp.bfloat16


def matmul(a, b, dims):
    return lax.dot_general(a, b, dims, preferred_element_type=F32)


def split(x):
    hi = x.astype(BF16)
    return hi, (x - hi.astype(F32)).astype(BF16)


def lane_low(shape):
    return lax.broadcasted_iota(jnp.int32, shape, len(shape) - 1) < LANES // 2


def half_roll(x):
    return pltpu.roll(x, LANES // 2, 1)


def far_first(count):
    return sorted(range(1, count), key=lambda k: -min(k, count - k))


def tree_sum(parts):
    while len(parts) > 1:
        parts = [parts[i] + parts[i + 1] if i + 1 < len(parts) else parts[i] for i in range(0, len(parts), 2)]
    return parts[0]


def widest(parts):
    parts = [jnp.abs(p[i:i + 8, q:q + LANES]) for p in parts for i in range(0, p.shape[0], 8) for q in range(0, p.shape[1], LANES)]
    while len(parts) > 1:
        parts = [jnp.maximum(*parts[i:i + 2]) if i + 1 < len(parts) else parts[i] for i in range(0, len(parts), 2)]
    return jnp.max(parts[0], axis=(0, 1), keepdims=True)


def scale_of(parts):
    e = jnp.ceil(jnp.log2(jnp.maximum(widest(parts), TINY)) * STEPS)
    return jnp.broadcast_to(e.astype(jnp.int32), (1, LANES)), jnp.exp2(e * (-1.0 / STEPS)) * PEAK


def scale_from(row):
    return jnp.exp2(row.astype(F32) * (1.0 / STEPS)) * (1.0 / PEAK)


def to_words(top, bot, factor):
    a = jnp.round(top * factor).astype(jnp.int32)
    b = jnp.round(bot * factor).astype(jnp.int32)
    return (a << 16) | (b & 0xFFFF)


def from_words(w):
    return (w >> 16).astype(F32), ((w << 16) >> 16).astype(F32)


def kernel(
    nrow,
    ncol,
    res_hbm,
    ib_hbm,
    linv_hbm,
    basis_hbm,
    slots_hbm,
    coarse_hbm,
    out_ref,
    res_ref,
    ib_ref,
    slots_ref,
    outgoing,
    incoming,
    linv,
    basis,
    basis2,
    coarse,
    coarse_t,
    hot_in,
    hot_out,
    col1,
    row1,
    pieces,
    received,
    col2,
    sets,
    row2,
    lent,
    wide_hi,
    wide_lo,
    load_sem,
    halo_send,
    halo_recv,
    lend_send,
    lend_recv,
    bulk_send,
    bulk_recv,
):
    r = lax.axis_index("row")
    c = lax.axis_index("col")
    z, x = c // NX, lax.rem(c, NX)
    y, core = r // CORES, lax.rem(r, CORES)
    nz, ny = ncol // NX, nrow // CORES
    rhs = res_ref.shape[0]
    own = res_ref.shape[1]
    half = rhs // 2
    quarter = rhs // 4
    rows, width = coarse.shape
    nev = basis.shape[0]
    low = lane_low((quarter, LANES))
    low1 = lane_low((1, LANES))

    col_offsets = sorted(
        ((dz, dx) for dz in range(nz) for dx in range(NX) if (dz, dx) != (0, 0)),
        key=lambda o: -(min(o[0], nz - o[0]) + min(o[1], NX - o[1])))
    row_offsets = sorted(
        ((dy, dk) for dy in range(ny) for dk in range(CORES) if (dy, dk) != (0, 0)),
        key=lambda o: -(min(o[0], ny - o[0]) + 0.5 * o[1]))

    def col_at(dz, dx):
        return lax.rem(z + dz, nz) * NX + lax.rem(x + dx, NX)

    def row_at(dy, dk):
        return lax.rem(y + dy, ny) * CORES + lax.rem(core + dk, CORES)

    exists = [r < nrow - 1, r > 0, c < ncol - 1, c > 0]
    target = [(r + 1, c), (r - 1, c), (r, c + 1), (r, c - 1)]
    opposite = [1, 0, 3, 2]

    barrier = pltpu.get_barrier_semaphore()
    for offset in col_offsets:
        pl.semaphore_signal(barrier, inc=1, device_id=(r, col_at(*offset)), device_id_type=MESH)
    for offset in row_offsets:
        pl.semaphore_signal(barrier, inc=1, device_id=(row_at(*offset), c), device_id_type=MESH)

    loads = [
        pltpu.make_async_copy(basis_hbm, basis, load_sem.at[0]),
        pltpu.make_async_copy(coarse_hbm, coarse, load_sem.at[1]),
        pltpu.make_async_copy(linv_hbm, linv, load_sem.at[2]),
        pltpu.make_async_copy(res_hbm, res_ref, load_sem.at[3]),
        pltpu.make_async_copy(ib_hbm, ib_ref, load_sem.at[4]),
        pltpu.make_async_copy(slots_hbm, slots_ref, load_sem.at[5]),
    ]
    for i in (3, 4, 0, 5, 1, 2):
        loads[i].start()
    loads[4].wait()
    loads[3].wait()

    blocks = [res_ref[:, b * BLK:(b + 1) * BLK] for b in range(own // BLK)]
    for d in range(4):
        index = ib_ref[0, d]
        value = blocks[0]
        for b in range(1, len(blocks)):
            value = jnp.where(index == b, blocks[b], value)
        outgoing[d] = value

        @pl.when(jnp.logical_not(exists[opposite[d]]))
        def _():
            incoming[d] = jnp.zeros_like(incoming[d])

        @pl.when(jnp.logical_not(exists[d]))
        def _():
            lent[d] = jnp.zeros_like(lent[d])

    def halo(d):
        return pltpu.make_async_remote_copy(
            src_ref=outgoing.at[d], dst_ref=incoming.at[d],
            send_sem=halo_send.at[d], recv_sem=halo_recv.at[d],
            device_id=target[d], device_id_type=MESH)

    def lend(d):
        return pltpu.make_async_remote_copy(
            src_ref=basis.at[:, pl.ds(own + d * BLK, BLK)], dst_ref=lent.at[d],
            send_sem=lend_send.at[d], recv_sem=lend_recv.at[d],
            device_id=target[opposite[d]], device_id_type=MESH)

    def send(phase, src, dst, device):
        pltpu.make_async_remote_copy(
            src_ref=src, dst_ref=dst, send_sem=bulk_send.at[phase], recv_sem=bulk_recv.at[phase],
            device_id=device, device_id_type=MESH).start()

    def arrived(phase, buf, count):
        some = buf.at[pl.ds(0, count)]
        pltpu.make_async_copy(some, some, bulk_recv.at[phase]).wait()

    def drained(phase, buf, count):
        some = buf.at[pl.ds(0, count)]
        pltpu.make_async_copy(some, some, bulk_send.at[phase]).wait()

    def spread_col(phase, buf, top, bot):
        row, factor = scale_of([top, bot])
        buf[c, :quarter] = to_words(top, bot, factor)
        buf[c, quarter:] = row
        for offset in col_offsets:
            send(phase, buf.at[c], buf.at[c], (r, col_at(*offset)))

    def gathered(buf):
        columns = []
        for p in range(ncol // 2):
            a, b = buf[2 * p, :quarter], buf[2 * p + 1, :quarter]
            scale = scale_from(jnp.where(low1, buf[2 * p, quarter:], buf[2 * p + 1, quarter:]))
            quarters = from_words(jnp.where(low, a, half_roll(b))) + from_words(jnp.where(low, half_roll(a), b))
            columns.append(jnp.concatenate([q * scale for q in quarters], axis=0))
        return jnp.concatenate(split(jnp.concatenate(columns, axis=1)), axis=0)

    def paired_words(part, factor):
        first = to_words(part[:quarter], part[quarter:half], factor)
        second = to_words(part[half:half + quarter], part[half + quarter:], factor)
        return jnp.where(low, first, half_roll(second)), jnp.where(low, half_roll(first), second)

    pl.semaphore_wait(barrier, ncol + nrow - 2)
    for d in range(4):
        @pl.when(exists[d])
        def _():
            halo(d).start()

    loads[5].wait()
    chunk = 2 * LANES
    place_in = lax.broadcasted_iota(jnp.int32, (width, chunk), 0) + c * width

    def build_in(i, carry):
        slot = slots_ref[:, pl.ds(pl.multiple_of(r * rows + i * chunk, chunk), chunk)]
        hot = jnp.where(place_in == slot, 1.0, 0.0).astype(BF16)
        hot_in[pl.ds(pl.multiple_of(i * chunk, chunk), chunk)] = hot.T
        return carry

    lax.fori_loop(0, rows // chunk, build_in, 0)
    loads[0].wait()
    b_hi, b_lo = split(basis[...])
    basis2[:nev] = b_hi
    basis2[nev:] = b_lo
    partial = matmul(res_ref[...], basis2[:, :own], NT)

    for d in range(4):
        @pl.when(exists[opposite[d]])
        def _():
            halo(d).wait_recv()

    inc = jnp.concatenate([incoming[d] for d in range(4)], axis=1)
    partial = partial + matmul(inc, basis2[:, own:], NT)
    partial = partial + half_roll(partial)
    spread_col(0, col1, jnp.where(low, partial[:quarter], partial[half:half + quarter]),
               jnp.where(low, partial[quarter:half], partial[half + quarter:]))

    span = rows // nz
    loads[1].wait()
    for t in range(nz):
        at = slice(t * span, (t + 1) * span)
        coarse_t[:width, at], coarse_t[width:, at] = split(coarse[at].T)
    loads[2].wait()
    local = jnp.concatenate([res_ref[...], inc], axis=1)
    out_ref[...] = matmul(local, linv[...], NT)

    arrived(0, col1, ncol - 1)
    part = matmul(gathered(col1), hot_in[...], NN)
    part = part[:rhs] + part[rhs:]
    row, factor = scale_of([part])
    blocks4 = width // LANES
    for q in range(blocks4):
        at = slice(q * LANES, (q + 1) * LANES)
        row1[r, q * half:(q + 1) * half] = to_words(part[:half, at], part[half:, at], factor)
    row1[r, blocks4 * half:] = row
    for offset in row_offsets:
        send(1, row1.at[r], row1.at[r], (row_at(*offset), c))

    low8 = lane_low((8, LANES))
    wanted = []
    for column, valid in ((c, None), (c + 1, exists[2]), (c - 1, exists[3])):
        safe = jnp.clip(column, 0, ncol - 1)
        for t in range(nrow // 2):
            pair = []
            for device in (2 * t * ncol + safe, (2 * t + 1) * ncol + safe):
                at = pl.ds(pl.multiple_of((device // 2) * LANES, LANES), LANES)
                pair.append(jnp.broadcast_to(slots_ref[:, at], (8, LANES)))
            even = jnp.where(low8, pair[0], half_roll(pair[1]))
            odd = jnp.where(low8, half_roll(pair[0]), pair[1])
            both = jnp.where(lax.rem(safe, 2) == 0, even, odd)[:1]
            wanted.append(both if valid is None else jnp.where(valid, both, -1))
    wanted = jnp.concatenate(wanted, axis=1) - r * rows
    place_out = lax.broadcasted_iota(jnp.int32, (LANES, wanted.shape[1]), 0)

    def build_out(i, carry):
        hot = jnp.where(place_out == wanted - i * LANES, 1.0, 0.0)
        hot_out[pl.ds(pl.multiple_of(i * LANES, LANES), LANES)] = hot.astype(BF16)
        return carry

    lax.fori_loop(0, rows // LANES, build_out, 0)

    arrived(1, row1, nrow - 1)
    scales = [scale_from(row1[i, blocks4 * half:]) for i in range(nrow)]
    column = []
    for q in range(blocks4):
        tops, bots = [], []
        for i in range(nrow):
            top, bot = from_words(row1[i, q * half:(q + 1) * half])
            tops.append(top * scales[i])
            bots.append(bot * scales[i])
        column.append(jnp.concatenate([tree_sum(tops), tree_sum(bots)], axis=0))
    column2 = jnp.concatenate(split(jnp.concatenate(column, axis=1)), axis=0)
    column4 = jnp.concatenate([column2, column2], axis=1)

    steps = far_first(nz) + [0]
    for batch in (steps[:nz // 2], steps[nz // 2:]):
        parts = []
        for dz in batch:
            block = lax.rem(z + dz, nz)
            at = pl.ds(pl.multiple_of(block * span, span), span)
            part = matmul(column4, coarse_t[:, at], NN)
            parts.append((block, part[:rhs] + part[rhs:]))
        row, factor = scale_of([part for block, part in parts])
        for block, part in parts:
            for q in range(span // LANES):
                pair = paired_words(part[:, q * LANES:(q + 1) * LANES], factor)
                for i in range(2):
                    pieces[block * NX + 2 * q + i, :quarter] = pair[i]
                    pieces[block * NX + 2 * q + i, quarter:] = row
        for dz, (block, part) in zip(batch, parts):
            for dx in (2, 1, 3, 0) if dz else (2, 1, 3):
                to = block * NX + lax.rem(x + dx, NX)
                send(2, pieces.at[to], received.at[c], (r, to))

    for d in range(4):
        @pl.when(exists[opposite[d]])
        def _():
            lend(d).start()

    received[c] = pieces[c]
    arrived(2, received, ncol - 1)
    tops, bots = [], []
    for i in range(ncol):
        scale = scale_from(received[i, quarter:])
        top, bot = from_words(received[i, :quarter])
        tops.append(top * scale)
        bots.append(bot * scale)
    top, bot = tree_sum(tops), tree_sum(bots)
    spread_col(3, col2, top, bot)

    wide_hi[:nev] = basis2[:nev, :own]
    wide_lo[:nev] = basis2[nev:, :own]
    wide_hi[5 * nev:] = jnp.zeros_like(wide_hi[5 * nev:])
    wide_lo[5 * nev:] = jnp.zeros_like(wide_lo[5 * nev:])
    for d in range(4):
        @pl.when(exists[d])
        def _():
            lend(d).wait_recv()

        l_hi, l_lo = split(lent[d])
        for b in range(own // BLK):
            here = ib_ref[0, d] == b
            at = slice((d + 1) * nev, (d + 2) * nev), slice(b * BLK, (b + 1) * BLK)
            wide_hi[at] = jnp.where(here, l_hi, jnp.zeros_like(l_hi))
            wide_lo[at] = jnp.where(here, l_lo, jnp.zeros_like(l_lo))

    arrived(3, col2, ncol - 1)
    part = matmul(gathered(col2), hot_out[...], NN)
    part = part[:rhs] + part[rhs:]
    row, factor = scale_of([part])
    words = []
    for q in range(part.shape[1] // LANES):
        words.extend(paired_words(part[:, q * LANES:(q + 1) * LANES], factor))
    for i in range(nrow):
        near = (i, min(i + 1, nrow - 1), max(i - 1, 0), nrow + i, 2 * nrow + i)
        for k, index in enumerate(near):
            sets[i, k * quarter:(k + 1) * quarter] = words[index]
        sets[i, 5 * quarter:] = row
    for offset in row_offsets:
        to = row_at(*offset)
        send(4, sets.at[to], row2.at[r], (to, c))
    row2[r] = sets[r]
    arrived(4, row2, nrow - 1)
    scales = [scale_from(row2[i, 5 * quarter:]) for i in range(nrow)]
    picks = []
    for k in range(5):
        tops, bots = [], []
        for i in range(nrow):
            top, bot = from_words(row2[i, k * quarter:(k + 1) * quarter])
            tops.append(top * scales[i])
            bots.append(bot * scales[i])
        picks.append((tree_sum(tops), tree_sum(bots)))
    picks.append((jnp.zeros_like(picks[0][0]),) * 2)
    columns = []
    for p in range(3):
        a, b = picks[2 * p], picks[2 * p + 1]
        columns.append(jnp.concatenate(
            [jnp.where(low, a[i], half_roll(b[i])) for i in range(2)]
            + [jnp.where(low, half_roll(a[i]), b[i]) for i in range(2)], axis=0))
    picked = jnp.concatenate(split(jnp.concatenate(columns, axis=1)), axis=0)
    inner = matmul(picked, wide_hi[...], NN) + matmul(picked, wide_lo[...], NN)
    out_ref[...] = out_ref[...] + inner[:rhs] + inner[rhs:]

    drained(0, col1, ncol - 1)
    drained(1, row1, nrow - 1)
    drained(2, received, ncol - 1)
    drained(3, col2, ncol - 1)
    drained(4, row2, nrow - 1)
    for d in range(4):
        @pl.when(exists[d])
        def _():
            halo(d).wait_send()

        @pl.when(exists[opposite[d]])
        def _():
            lend(d).wait_send()


def shards(nrow, ncol, residuals, intersect_blocks, local_inverse, coarse_basis, coarse_slots, coarse_inverse):
    own, rhs = residuals.shape
    loc, nev = coarse_basis.shape
    rows, width = coarse_inverse.shape
    total = coarse_slots.shape[0]
    assert 2 * nev == LANES and rows == ncol * nev and width == nrow * nev and loc == own + 4 * BLK and own % BLK == 0
    vmem = pl.BlockSpec(memory_space=pltpu.VMEM)
    hbm = pl.BlockSpec(memory_space=pl.ANY)
    dma = pltpu.SemaphoreType.DMA
    out = pl.pallas_call(
        functools.partial(kernel, nrow, ncol),
        name="schwarz",
        out_shape=pltpu.VMEM((rhs, own), F32),
        in_specs=[hbm] * 6,
        out_specs=vmem,
        scratch_shapes=[
            pltpu.VMEM((rhs, own), BF16),
            pltpu.SMEM(intersect_blocks.shape, jnp.int32),
            pltpu.VMEM((1, total), jnp.int32),
            pltpu.VMEM((4, rhs, BLK), BF16),
            pltpu.VMEM((4, rhs, BLK), BF16),
            pltpu.VMEM((own, loc), BF16),
            pltpu.VMEM((nev, loc), F32),
            pltpu.VMEM((2 * nev, loc), BF16),
            pltpu.VMEM((rows, width), F32),
            pltpu.VMEM((2 * width, rows), BF16),
            pltpu.VMEM((rows, width), BF16),
            pltpu.VMEM((rows, 3 * width), BF16),
            pltpu.VMEM((ncol, rhs // 4 + 1, LANES), jnp.int32),
            pltpu.VMEM((nrow, width // LANES * (rhs // 2) + 1, LANES), jnp.int32),
            pltpu.VMEM((ncol, rhs // 4 + 1, LANES), jnp.int32),
            pltpu.VMEM((ncol, rhs // 4 + 1, LANES), jnp.int32),
            pltpu.VMEM((ncol, rhs // 4 + 1, LANES), jnp.int32),
            pltpu.VMEM((nrow, 5 * (rhs // 4) + 1, LANES), jnp.int32),
            pltpu.VMEM((nrow, 5 * (rhs // 4) + 1, LANES), jnp.int32),
            pltpu.VMEM((4, nev, BLK), F32),
            pltpu.VMEM((6 * nev, own), BF16),
            pltpu.VMEM((6 * nev, own), BF16),
            dma((6,)),
            dma((4,)),
            dma((4,)),
            dma((4,)),
            dma((4,)),
            dma((5,)),
            dma((5,)),
        ],
        compiler_params=pltpu.CompilerParams(collective_id=0, has_side_effects=True),
    )(
        residuals.T,
        intersect_blocks,
        local_inverse,
        coarse_basis.T,
        coarse_slots.reshape(1, total),
        coarse_inverse,
    )
    return out.T


def solution(mesh):
    placed = (
        P(("row", "col"), None),
        P(("row", "col"), None),
        P(("row", "col"), None),
        P(("row", "col"), None),
        P(),
        P("row", "col"),
    )
    return jax.shard_map(
        functools.partial(shards, mesh.shape["row"], mesh.shape["col"]),
        mesh=mesh, in_specs=placed, out_specs=P(("row", "col"), None), check_vma=False,
    )
```

time: 52.7 us -> 47 us (0.89)
  Pallas kernels: 52 us -> 46.2 us
    pallas_call x1, Pallas kernels: 52 us -> 46.2 us  [shards(): pl.pallas_call(functools.partial(kernel, nrow, ncol), name='schwarz', out...]
where the time goes in v3:
time: 47 us; the launch traced here: 46.9 us
  Pallas kernels  46.2 us (98%)
  local copies, waits for them, and re-layouts  0.63 us (1%)
    pallas_call x1, Pallas kernels, shards(): pl.pallas_call(functools.partial(kernel, nrow, ncol), name='schwarz', out...  46.2 us

profile of v3, /device:TPU:1, one launch (start us, length us, event | category | flops | bytes accessed | tf_op | source)
XLA Modules:
  0.0 46.9 jit_solution(7876831180149010344)
XLA Ops:
  0.0 46.2 %schwarz.1 = f32[32,512]{1,0:T(8,128)S(1)} custom-call(bf16[32,512]{1,0:T(8,128)(2,1)} %bitcast.7, s32[1,4]{1,0:T(1,128)} %ib_hbm.1, bf16[512,1024]{1,0:T(8,128)(2,1)} %linv_hbm.1, f32[64,1024]{1,0:T(8,128)} %bitcast.5, s32[1,16384]{1,0:T(1,128)} %bitcast.6, f32[2048,512]{1,0:T(8,128)} %coarse_hbm.1), custom_call_target="tpu_custom_call" | custom-call | tf_op jit(solution)/shard_map/schwarz/pallas_call | solution.py:433
  46.3 0.6 %copy.8 = f32[512,32]{0,1:T(8,128)} copy(f32[512,32]{0,1:T(8,128)S(1)} %bitcast.4) | data formatting | bytes 131072

commit v4 on v3

--- a/solution.py
+++ b/solution.py
@@ -48,16 +48,10 @@
     return parts[0]
 
 
-def widest(parts):
-    parts = [jnp.abs(p[i:i + 8, q:q + LANES]) for p in parts for i in range(0, p.shape[0], 8) for q in range(0, p.shape[1], LANES)]
-    while len(parts) > 1:
-        parts = [jnp.maximum(*parts[i:i + 2]) if i + 1 < len(parts) else parts[i] for i in range(0, len(parts), 2)]
-    return jnp.max(parts[0], axis=(0, 1), keepdims=True)
-
-
-def scale_of(parts):
-    e = jnp.ceil(jnp.log2(jnp.maximum(widest(parts), TINY)) * STEPS)
-    return jnp.broadcast_to(e.astype(jnp.int32), (1, LANES)), jnp.exp2(e * (-1.0 / STEPS)) * PEAK
+def scale_of(largest):
+    top = jnp.broadcast_to(jnp.max(largest, axis=0, keepdims=True), largest.shape)
+    e = jnp.ceil(jnp.log2(jnp.maximum(top, TINY)) * STEPS)
+    return e.astype(jnp.int32), jnp.exp2(e * (-1.0 / STEPS)) * PEAK
 
 
 def scale_from(row):
@@ -113,6 +107,7 @@
     lend_recv,
     bulk_send,
     bulk_recv,
+    passed,
 ):
     r = lax.axis_index("row")
     c = lax.axis_index("col")
@@ -145,12 +140,6 @@
     target = [(r + 1, c), (r - 1, c), (r, c + 1), (r, c - 1)]
     opposite = [1, 0, 3, 2]
 
-    barrier = pltpu.get_barrier_semaphore()
-    for offset in col_offsets:
-        pl.semaphore_signal(barrier, inc=1, device_id=(r, col_at(*offset)), device_id_type=MESH)
-    for offset in row_offsets:
-        pl.semaphore_signal(barrier, inc=1, device_id=(row_at(*offset), c), device_id_type=MESH)
-
     loads = [
         pltpu.make_async_copy(basis_hbm, basis, load_sem.at[0]),
         pltpu.make_async_copy(coarse_hbm, coarse, load_sem.at[1]),
@@ -159,7 +148,37 @@
         pltpu.make_async_copy(ib_hbm, ib_ref, load_sem.at[4]),
         pltpu.make_async_copy(slots_hbm, slots_ref, load_sem.at[5]),
     ]
-    for i in (3, 4, 0, 5, 1, 2):
+    for i in (3, 4, 0):
+        loads[i].start()
+
+    def line_x(dx):
+        return (r, z * NX + lax.rem(x + dx, NX))
+
+    def line_z(dz):
+        return (r, lax.rem(z + dz, nz) * NX + x)
+
+    across_x = [line_x(dx) for dx in (1, NX - 1, 2)]
+    near_z = [line_z(dz) for dz in (1, nz - 1, 2, nz - 2)]
+    up = jnp.logical_and(x == NX - 1, exists[2])
+    down = jnp.logical_and(x == 0, exists[3])
+    barrier = pltpu.get_barrier_semaphore()
+
+    def signal(sem, device):
+        pl.semaphore_signal(sem, inc=1, device_id=device, device_id_type=MESH)
+
+    @pl.when(up)
+    def _():
+        signal(barrier, target[2])
+
+    @pl.when(down)
+    def _():
+        signal(barrier, target[3])
+
+    for offset in row_offsets:
+        signal(barrier, (row_at(*offset), c))
+    for device in across_x + near_z:
+        signal(barrier, device)
+    for i in (5, 1, 2):
         loads[i].start()
     loads[4].wait()
     loads[3].wait()
@@ -205,49 +224,69 @@
         some = buf.at[pl.ds(0, count)]
         pltpu.make_async_copy(some, some, bulk_send.at[phase]).wait()
 
-    def spread_col(phase, buf, top, bot):
-        row, factor = scale_of([top, bot])
+    plane = NX * nev
+    near = 5
+
+    def plane_at(k):
+        return lax.rem(z + (k + 1) // 2 * (2 * (k % 2) - 1) + nz, nz)
+
+    def is_far(dz):
+        return min(dz, nz - dz) > near // 2
+
+    def spread_col(phase, buf, top, bot, ready):
+        largest = jnp.maximum(jnp.abs(top), jnp.abs(bot))
+        e, factor = scale_of(jnp.maximum(largest, half_roll(largest)))
         buf[c, :quarter] = to_words(top, bot, factor)
-        buf[c, quarter:] = row
-        for offset in col_offsets:
-            send(phase, buf.at[c], buf.at[c], (r, col_at(*offset)))
-
-    def gathered(buf):
+        buf[c, quarter:] = e[:1]
+        ready()
+        for dz, dx in col_offsets:
+            send(phase + is_far(dz), buf.at[c], buf.at[c], (r, col_at(dz, dx)))
+
+    def gathered(buf, planes):
         columns = []
-        for p in range(ncol // 2):
-            a, b = buf[2 * p, :quarter], buf[2 * p + 1, :quarter]
-            scale = scale_from(jnp.where(low1, buf[2 * p, quarter:], buf[2 * p + 1, quarter:]))
-            quarters = from_words(jnp.where(low, a, half_roll(b))) + from_words(jnp.where(low, half_roll(a), b))
-            columns.append(jnp.concatenate([q * scale for q in quarters], axis=0))
+        for k in planes:
+            for q in range(0, NX, 2):
+                first = plane_at(k) * NX + q
+                a, b = buf[first, :quarter], buf[first + 1, :quarter]
+                scale = scale_from(jnp.where(low1, buf[first, quarter:], buf[first + 1, quarter:]))
+                quarters = from_words(jnp.where(low, a, half_roll(b))) + from_words(jnp.where(low, half_roll(a), b))
+                columns.append(jnp.concatenate([v * scale for v in quarters], axis=0))
         return jnp.concatenate(split(jnp.concatenate(columns, axis=1)), axis=0)
 
-    def paired_words(part, factor):
+    def select(phase, buf, hot):
+        arrived(phase, buf, near * NX - 1)
+        part = matmul(gathered(buf, range(near)), hot[:near * plane], NN)
+        arrived(phase + 1, buf, (nz - near) * NX)
+        part = part + matmul(gathered(buf, range(near, nz)), hot[near * plane:], NN)
+        return part[:rhs] + part[rhs:]
+
+    def largest_of(part):
+        return functools.reduce(jnp.maximum, [jnp.abs(part[i:i + quarter]) for i in range(0, rhs, quarter)])
+
+    def paired_words(part):
+        e, factor = scale_of(largest_of(part))
         first = to_words(part[:quarter], part[quarter:half], factor)
         second = to_words(part[half:half + quarter], part[half + quarter:], factor)
-        return jnp.where(low, first, half_roll(second)), jnp.where(low, half_roll(first), second)
-
-    pl.semaphore_wait(barrier, ncol + nrow - 2)
+        swapped = half_roll(e)
+        return ((jnp.where(low, first, half_roll(second)), jnp.where(low, e, swapped)[:1]),
+                (jnp.where(low, half_roll(first), second), jnp.where(low, swapped, e)[:1]))
+
+    pl.semaphore_wait(barrier, nrow - 1 + len(across_x) + len(near_z) + up.astype(jnp.int32) + down.astype(jnp.int32))
     for d in range(4):
         @pl.when(exists[d])
         def _():
             halo(d).start()
 
-    loads[5].wait()
-    chunk = 2 * LANES
-    place_in = lax.broadcasted_iota(jnp.int32, (width, chunk), 0) + c * width
-
-    def build_in(i, carry):
-        slot = slots_ref[:, pl.ds(pl.multiple_of(r * rows + i * chunk, chunk), chunk)]
-        hot = jnp.where(place_in == slot, 1.0, 0.0).astype(BF16)
-        hot_in[pl.ds(pl.multiple_of(i * chunk, chunk), chunk)] = hot.T
-        return carry
-
-    lax.fori_loop(0, rows // chunk, build_in, 0)
+    for device in across_x + near_z:
+        signal(passed.at[0], device)
     loads[0].wait()
     b_hi, b_lo = split(basis[...])
     basis2[:nev] = b_hi
     basis2[nev:] = b_lo
     partial = matmul(res_ref[...], basis2[:, :own], NT)
+    pl.semaphore_wait(passed.at[0], len(across_x) + len(near_z))
+    for device in across_x:
+        signal(passed.at[1], device)
 
     for d in range(4):
         @pl.when(exists[opposite[d]])
@@ -258,7 +297,8 @@
     partial = partial + matmul(inc, basis2[:, own:], NT)
     partial = partial + half_roll(partial)
     spread_col(0, col1, jnp.where(low, partial[:quarter], partial[half:half + quarter]),
-               jnp.where(low, partial[quarter:half], partial[half + quarter:]))
+               jnp.where(low, partial[quarter:half], partial[half + quarter:]),
+               lambda: pl.semaphore_wait(passed.at[1], len(across_x)))
 
     span = rows // nz
     loads[1].wait()
@@ -269,17 +309,26 @@
     local = jnp.concatenate([res_ref[...], inc], axis=1)
     out_ref[...] = matmul(local, linv[...], NT)
 
-    arrived(0, col1, ncol - 1)
-    part = matmul(gathered(col1), hot_in[...], NN)
-    part = part[:rhs] + part[rhs:]
-    row, factor = scale_of([part])
+    loads[5].wait()
+    place_in = lax.broadcasted_iota(jnp.int32, (width, plane), 0) + c * width
+
+    def build_in(k, carry):
+        slot = slots_ref[:, pl.ds(pl.multiple_of(r * rows + plane_at(k) * plane, plane), plane)]
+        hot = jnp.where(place_in == slot, 1.0, 0.0).astype(BF16)
+        hot_in[pl.ds(pl.multiple_of(k * plane, plane), plane)] = hot.T
+        return carry
+
+    lax.fori_loop(0, nz, build_in, 0)
+
+    part = select(0, col1, hot_in)
     blocks4 = width // LANES
     for q in range(blocks4):
-        at = slice(q * LANES, (q + 1) * LANES)
-        row1[r, q * half:(q + 1) * half] = to_words(part[:half, at], part[half:, at], factor)
-    row1[r, blocks4 * half:] = row
+        block = part[:, q * LANES:(q + 1) * LANES]
+        e, factor = scale_of(largest_of(block))
+        row1[r, q * half:(q + 1) * half] = to_words(block[:half], block[half:], factor[:1])
+        row1[r, blocks4 * half + q:blocks4 * half + q + 1] = e[:1]
     for offset in row_offsets:
-        send(1, row1.at[r], row1.at[r], (row_at(*offset), c))
+        send(2, row1.at[r], row1.at[r], (row_at(*offset), c))
 
     low8 = lane_low((8, LANES))
     wanted = []
@@ -298,44 +347,43 @@
     place_out = lax.broadcasted_iota(jnp.int32, (LANES, wanted.shape[1]), 0)
 
     def build_out(i, carry):
-        hot = jnp.where(place_out == wanted - i * LANES, 1.0, 0.0)
+        start = plane_at(i // 2) * plane + i % 2 * LANES
+        hot = jnp.where(place_out == wanted - start, 1.0, 0.0)
         hot_out[pl.ds(pl.multiple_of(i * LANES, LANES), LANES)] = hot.astype(BF16)
         return carry
 
     lax.fori_loop(0, rows // LANES, build_out, 0)
 
-    arrived(1, row1, nrow - 1)
-    scales = [scale_from(row1[i, blocks4 * half:]) for i in range(nrow)]
+    arrived(2, row1, nrow - 1)
     column = []
     for q in range(blocks4):
         tops, bots = [], []
         for i in range(nrow):
+            scale = scale_from(row1[i, blocks4 * half + q:blocks4 * half + q + 1])
             top, bot = from_words(row1[i, q * half:(q + 1) * half])
-            tops.append(top * scales[i])
-            bots.append(bot * scales[i])
+            tops.append(top * scale)
+            bots.append(bot * scale)
         column.append(jnp.concatenate([tree_sum(tops), tree_sum(bots)], axis=0))
     column2 = jnp.concatenate(split(jnp.concatenate(column, axis=1)), axis=0)
     column4 = jnp.concatenate([column2, column2], axis=1)
 
     steps = far_first(nz) + [0]
-    for batch in (steps[:nz // 2], steps[nz // 2:]):
+    for batch in (steps[:2], steps[2:5], steps[5:]):
         parts = []
         for dz in batch:
             block = lax.rem(z + dz, nz)
             at = pl.ds(pl.multiple_of(block * span, span), span)
             part = matmul(column4, coarse_t[:, at], NN)
             parts.append((block, part[:rhs] + part[rhs:]))
-        row, factor = scale_of([part for block, part in parts])
         for block, part in parts:
             for q in range(span // LANES):
-                pair = paired_words(part[:, q * LANES:(q + 1) * LANES], factor)
-                for i in range(2):
-                    pieces[block * NX + 2 * q + i, :quarter] = pair[i]
-                    pieces[block * NX + 2 * q + i, quarter:] = row
+                for i, (words, e) in enumerate(paired_words(part[:, q * LANES:(q + 1) * LANES])):
+                    pieces[block * NX + 2 * q + i, :quarter] = words
+                    pieces[block * NX + 2 * q + i, quarter:] = e
         for dz, (block, part) in zip(batch, parts):
             for dx in (2, 1, 3, 0) if dz else (2, 1, 3):
                 to = block * NX + lax.rem(x + dx, NX)
-                send(2, pieces.at[to], received.at[c], (r, to))
+                send(3, pieces.at[to], received.at[c], (r, to))
 
     for d in range(4):
         @pl.when(exists[opposite[d]])
@@ -343,7 +391,7 @@
             lend(d).start()
 
     received[c] = pieces[c]
-    arrived(2, received, ncol - 1)
+    arrived(3, received, ncol - 1)
     tops, bots = [], []
     for i in range(ncol):
         scale = scale_from(received[i, quarter:])
@@ -351,7 +399,7 @@
         tops.append(top * scale)
         bots.append(bot * scale)
     top, bot = tree_sum(tops), tree_sum(bots)
-    spread_col(3, col2, top, bot)
+    spread_col(4, col2, top, bot, lambda: None)
 
     wide_hi[:nev] = basis2[:nev, :own]
     wide_lo[:nev] = basis2[nev:, :own]
@@ -369,31 +417,27 @@
             wide_hi[at] = jnp.where(here, l_hi, jnp.zeros_like(l_hi))
             wide_lo[at] = jnp.where(here, l_lo, jnp.zeros_like(l_lo))
 
-    arrived(3, col2, ncol - 1)
-    part = matmul(gathered(col2), hot_out[...], NN)
-    part = part[:rhs] + part[rhs:]
-    row, factor = scale_of([part])
-    words = []
+    part = select(4, col2, hot_out)
+    groups = []
     for q in range(part.shape[1] // LANES):
-        words.extend(paired_words(part[:, q * LANES:(q + 1) * LANES], factor))
+        groups.extend(paired_words(part[:, q * LANES:(q + 1) * LANES]))
     for i in range(nrow):
-        near = (i, min(i + 1, nrow - 1), max(i - 1, 0), nrow + i, 2 * nrow + i)
-        for k, index in enumerate(near):
-            sets[i, k * quarter:(k + 1) * quarter] = words[index]
-        sets[i, 5 * quarter:] = row
+        around = (i, min(i + 1, nrow - 1), max(i - 1, 0), nrow + i, 2 * nrow + i)
+        for k, index in enumerate(around):
+            sets[i, k * quarter:(k + 1) * quarter], sets[i, 5 * quarter + k:5 * quarter + k + 1] = groups[index]
     for offset in row_offsets:
         to = row_at(*offset)
-        send(4, sets.at[to], row2.at[r], (to, c))
+        send(6, sets.at[to], row2.at[r], (to, c))
     row2[r] = sets[r]
-    arrived(4, row2, nrow - 1)
-    scales = [scale_from(row2[i, 5 * quarter:]) for i in range(nrow)]
+    arrived(6, row2, nrow - 1)
     picks = []
     for k in range(5):
         tops, bots = [], []
         for i in range(nrow):
+            scale = scale_from(row2[i, 5 * quarter + k:5 * quarter + k + 1])
             top, bot = from_words(row2[i, k * quarter:(k + 1) * quarter])
-            tops.append(top * scales[i])
-            bots.append(bot * scales[i])
+            tops.append(top * scale)
+            bots.append(bot * scale)
         picks.append((tree_sum(tops), tree_sum(bots)))
     picks.append((jnp.zeros_like(picks[0][0]),) * 2)
     columns = []
@@ -406,11 +450,12 @@
     inner = matmul(picked, wide_hi[...], NN) + matmul(picked, wide_lo[...], NN)
     out_ref[...] = out_ref[...] + inner[:rhs] + inner[rhs:]
 
-    drained(0, col1, ncol - 1)
-    drained(1, row1, nrow - 1)
-    drained(2, received, ncol - 1)
-    drained(3, col2, ncol - 1)
-    drained(4, row2, nrow - 1)
+    for phase, buf in ((0, col1), (4, col2)):
+        drained(phase, buf, near * NX - 1)
+        drained(phase + 1, buf, (nz - near) * NX)
+    drained(2, row1, nrow - 1)
+    drained(3, received, ncol - 1)
+    drained(6, row2, nrow - 1)
     for d in range(4):
         @pl.when(exists[d])
         def _():
@@ -450,12 +495,12 @@
             pltpu.VMEM((rows, width), BF16),
             pltpu.VMEM((rows, 3 * width), BF16),
             pltpu.VMEM((ncol, rhs // 4 + 1, LANES), jnp.int32),
-            pltpu.VMEM((nrow, width // LANES * (rhs // 2) + 1, LANES), jnp.int32),
+            pltpu.VMEM((nrow, width // LANES * (rhs // 2 + 1), LANES), jnp.int32),
             pltpu.VMEM((ncol, rhs // 4 + 1, LANES), jnp.int32),
             pltpu.VMEM((ncol, rhs // 4 + 1, LANES), jnp.int32),
             pltpu.VMEM((ncol, rhs // 4 + 1, LANES), jnp.int32),
-            pltpu.VMEM((nrow, 5 * (rhs // 4) + 1, LANES), jnp.int32),
-            pltpu.VMEM((nrow, 5 * (rhs // 4) + 1, LANES), jnp.int32),
+            pltpu.VMEM((nrow, 5 * (rhs // 4 + 1), LANES), jnp.int32),
+            pltpu.VMEM((nrow, 5 * (rhs // 4 + 1), LANES), jnp.int32),
             pltpu.VMEM((4, nev, BLK), F32),
             pltpu.VMEM((6 * nev, own), BF16),
             pltpu.VMEM((6 * nev, own), BF16),
@@ -464,8 +509,9 @@
             dma((4,)),
             dma((4,)),
             dma((4,)),
-            dma((5,)),
-            dma((5,)),
+            dma((7,)),
+            dma((7,)),
+            pltpu.SemaphoreType.REGULAR((2,)),
         ],
         compiler_params=pltpu.CompilerParams(collective_id=0, has_side_effects=True),
     )(

time: 47 us -> 45.4 us (0.966)
  Pallas kernels: 46.2 us -> 44.7 us
    pallas_call x1, Pallas kernels: 46.2 us -> 44.7 us  [shards(): pl.pallas_call(functools.partial(kernel, nrow, ncol), name='schwarz', out...]
where the time goes in v4:
time: 45.4 us
  Pallas kernels  44.7 us (98%)
  local copies, waits for them, and re-layouts  0.63 us (1%)
    pallas_call x1, Pallas kernels, shards(): pl.pallas_call(functools.partial(kernel, nrow, ncol), name='schwarz', out...  44.7 us

profile of v4, /device:TPU:1, one launch (start us, length us, event | category | flops | bytes accessed | tf_op | source)
XLA Modules:
  0.0 45.4 jit_solution(15692382453828067035)
XLA Ops:
  0.0 44.7 %schwarz.1 = f32[32,512]{1,0:T(8,128)S(1)} custom-call(bf16[32,512]{1,0:T(8,128)(2,1)} %bitcast.7, s32[1,4]{1,0:T(1,128)} %ib_hbm.1, bf16[512,1024]{1,0:T(8,128)(2,1)} %linv_hbm.1, f32[64,1024]{1,0:T(8,128)} %bitcast.5, s32[1,16384]{1,0:T(1,128)} %bitcast.6, f32[2048,512]{1,0:T(8,128)} %coarse_hbm.1), custom_call_target="tpu_custom_call" | custom-call | tf_op jit(solution)/shard_map/schwarz/pallas_call | solution.py:478
  44.7 0.6 %copy.8 = f32[512,32]{0,1:T(8,128)} copy(f32[512,32]{0,1:T(8,128)S(1)} %bitcast.4) | data formatting | bytes 131072

commit v5 on v4

--- a/solution.py
+++ b/solution.py
@@ -224,41 +224,23 @@
         some = buf.at[pl.ds(0, count)]
         pltpu.make_async_copy(some, some, bulk_send.at[phase]).wait()
 
-    plane = NX * nev
-    near = 5
-
-    def plane_at(k):
-        return lax.rem(z + (k + 1) // 2 * (2 * (k % 2) - 1) + nz, nz)
-
-    def is_far(dz):
-        return min(dz, nz - dz) > near // 2
-
     def spread_col(phase, buf, top, bot, ready):
         largest = jnp.maximum(jnp.abs(top), jnp.abs(bot))
         e, factor = scale_of(jnp.maximum(largest, half_roll(largest)))
         buf[c, :quarter] = to_words(top, bot, factor)
         buf[c, quarter:] = e[:1]
         ready()
-        for dz, dx in col_offsets:
-            send(phase + is_far(dz), buf.at[c], buf.at[c], (r, col_at(dz, dx)))
-
-    def gathered(buf, planes):
+        for offset in col_offsets:
+            send(phase, buf.at[c], buf.at[c], (r, col_at(*offset)))
+
+    def gathered(buf):
         columns = []
-        for k in planes:
-            for q in range(0, NX, 2):
-                first = plane_at(k) * NX + q
-                a, b = buf[first, :quarter], buf[first + 1, :quarter]
-                scale = scale_from(jnp.where(low1, buf[first, quarter:], buf[first + 1, quarter:]))
-                quarters = from_words(jnp.where(low, a, half_roll(b))) + from_words(jnp.where(low, half_roll(a), b))
-                columns.append(jnp.concatenate([v * scale for v in quarters], axis=0))
+        for first in range(0, ncol, 2):
+            a, b = buf[first, :quarter], buf[first + 1, :quarter]
+            scale = scale_from(jnp.where(low1, buf[first, quarter:], buf[first + 1, quarter:]))
+            quarters = from_words(jnp.where(low, a, half_roll(b))) + from_words(jnp.where(low, half_roll(a), b))
+            columns.append(jnp.concatenate([v * scale for v in quarters], axis=0))
         return jnp.concatenate(split(jnp.concatenate(columns, axis=1)), axis=0)
-
-    def select(phase, buf, hot):
-        arrived(phase, buf, near * NX - 1)
-        part = matmul(gathered(buf, range(near)), hot[:near * plane], NN)
-        arrived(phase + 1, buf, (nz - near) * NX)
-        part = part + matmul(gathered(buf, range(near, nz)), hot[near * plane:], NN)
-        return part[:rhs] + part[rhs:]
 
     def largest_of(part):
         return functools.reduce(jnp.maximum, [jnp.abs(part[i:i + quarter]) for i in range(0, rhs, quarter)])
@@ -310,17 +292,20 @@
     out_ref[...] = matmul(local, linv[...], NT)
 
     loads[5].wait()
-    place_in = lax.broadcasted_iota(jnp.int32, (width, plane), 0) + c * width
-
-    def build_in(k, carry):
-        slot = slots_ref[:, pl.ds(pl.multiple_of(r * rows + plane_at(k) * plane, plane), plane)]
+    chunk = 2 * LANES
+    place_in = lax.broadcasted_iota(jnp.int32, (width, chunk), 0) + c * width
+
+    def build_in(i, carry):
+        slot = slots_ref[:, pl.ds(pl.multiple_of(r * rows + i * chunk, chunk), chunk)]
         hot = jnp.where(place_in == slot, 1.0, 0.0).astype(BF16)
-        hot_in[pl.ds(pl.multiple_of(k * plane, plane), plane)] = hot.T
+        hot_in[pl.ds(pl.multiple_of(i * chunk, chunk), chunk)] = hot.T
         return carry
 
-    lax.fori_loop(0, nz, build_in, 0)
-
-    part = select(0, col1, hot_in)
+    lax.fori_loop(0, rows // chunk, build_in, 0)
+
+    arrived(0, col1, ncol - 1)
+    part = matmul(gathered(col1), hot_in[...], NN)
+    part = part[:rhs] + part[rhs:]
     blocks4 = width // LANES
     for q in range(blocks4):
         block = part[:, q * LANES:(q + 1) * LANES]
@@ -328,33 +313,36 @@
         row1[r, q * half:(q + 1) * half] = to_words(block[:half], block[half:], factor[:1])
         row1[r, blocks4 * half + q:blocks4 * half + q + 1] = e[:1]
     for offset in row_offsets:
-        send(2, row1.at[r], row1.at[r], (row_at(*offset), c))
-
+        send(1, row1.at[r], row1.at[r], (row_at(*offset), c))
+
+    order = [(0, dy) for dy in range(ny)] + [(side, dy) for dy in far_first(ny) + [0] for side in (1, -1)]
+    place = {key: i for i, key in enumerate(order)}
     low8 = lane_low((8, LANES))
     wanted = []
-    for column, valid in ((c, None), (c + 1, exists[2]), (c - 1, exists[3])):
-        safe = jnp.clip(column, 0, ncol - 1)
-        for t in range(nrow // 2):
-            pair = []
-            for device in (2 * t * ncol + safe, (2 * t + 1) * ncol + safe):
-                at = pl.ds(pl.multiple_of((device // 2) * LANES, LANES), LANES)
-                pair.append(jnp.broadcast_to(slots_ref[:, at], (8, LANES)))
-            even = jnp.where(low8, pair[0], half_roll(pair[1]))
-            odd = jnp.where(low8, half_roll(pair[0]), pair[1])
-            both = jnp.where(lax.rem(safe, 2) == 0, even, odd)[:1]
-            wanted.append(both if valid is None else jnp.where(valid, both, -1))
+    for side, dy in order:
+        safe = jnp.clip(c + side, 0, ncol - 1)
+        first = lax.rem(y + dy, ny) * CORES * ncol + safe
+        pair = []
+        for device in (first, first + ncol):
+            at = pl.ds(pl.multiple_of((device // 2) * LANES, LANES), LANES)
+            pair.append(jnp.broadcast_to(slots_ref[:, at], (8, LANES)))
+        even = jnp.where(low8, pair[0], half_roll(pair[1]))
+        odd = jnp.where(low8, half_roll(pair[0]), pair[1])
+        both = jnp.where(lax.rem(safe, 2) == 0, even, odd)[:1]
+        if side:
+            both = jnp.where(exists[2] if side > 0 else exists[3], both, -1)
+        wanted.append(both)
     wanted = jnp.concatenate(wanted, axis=1) - r * rows
     place_out = lax.broadcasted_iota(jnp.int32, (LANES, wanted.shape[1]), 0)
 
     def build_out(i, carry):
-        start = plane_at(i // 2) * plane + i % 2 * LANES
-        hot = jnp.where(place_out == wanted - start, 1.0, 0.0)
+        hot = jnp.where(place_out == wanted - i * LANES, 1.0, 0.0)
         hot_out[pl.ds(pl.multiple_of(i * LANES, LANES), LANES)] = hot.astype(BF16)
         return carry
 
     lax.fori_loop(0, rows // LANES, build_out, 0)
 
-    arrived(2, row1, nrow - 1)
+    arrived(1, row1, nrow - 1)
     column = []
     for q in range(blocks4):
         tops, bots = [], []
@@ -383,7 +371,7 @@
         for dz, (block, part) in zip(batch, parts):
             for dx in (2, 1, 3, 0) if dz else (2, 1, 3):
                 to = block * NX + lax.rem(x + dx, NX)
-                send(3, pieces.at[to], received.at[c], (r, to))
+                send(2, pieces.at[to], received.at[c], (r, to))
 
     for d in range(4):
         @pl.when(exists[opposite[d]])
@@ -391,7 +379,7 @@
             lend(d).start()
 
     received[c] = pieces[c]
-    arrived(3, received, ncol - 1)
+    arrived(2, received, ncol - 1)
     tops, bots = [], []
     for i in range(ncol):
         scale = scale_from(received[i, quarter:])
@@ -399,7 +387,7 @@
         tops.append(top * scale)
         bots.append(bot * scale)
     top, bot = tree_sum(tops), tree_sum(bots)
-    spread_col(4, col2, top, bot, lambda: None)
+    spread_col(3, col2, top, bot, lambda: None)
 
     wide_hi[:nev] = basis2[:nev, :own]
     wide_lo[:nev] = basis2[nev:, :own]
@@ -417,19 +405,33 @@
             wide_hi[at] = jnp.where(here, l_hi, jnp.zeros_like(l_hi))
             wide_lo[at] = jnp.where(here, l_lo, jnp.zeros_like(l_lo))
 
-    part = select(4, col2, hot_out)
+    arrived(3, col2, ncol - 1)
+    solution = gathered(col2)
     groups = []
-    for q in range(part.shape[1] // LANES):
-        groups.extend(paired_words(part[:, q * LANES:(q + 1) * LANES]))
-    for i in range(nrow):
-        around = (i, min(i + 1, nrow - 1), max(i - 1, 0), nrow + i, 2 * nrow + i)
-        for k, index in enumerate(around):
-            sets[i, k * quarter:(k + 1) * quarter], sets[i, 5 * quarter + k:5 * quarter + k + 1] = groups[index]
-    for offset in row_offsets:
-        to = row_at(*offset)
-        send(6, sets.at[to], row2.at[r], (to, c))
+    for dys, stop in (((2,), ny + 2), ((1, 3), ny + 6), ((0,), ny + 8)):
+        start = len(groups) // 2
+        part = matmul(solution, hot_out[:, start * LANES:stop * LANES], NN)
+        part = part[:rhs] + part[rhs:]
+        for q in range(stop - start):
+            groups.extend(paired_words(part[:, q * LANES:(q + 1) * LANES]))
+        for dy in dys:
+            for k in range(CORES):
+                up_row = (0, (dy + (k + 1) // CORES) % ny, (k + 1) % CORES)
+                down_row = (0, (dy + (k - 1) // CORES) % ny, (k - 1) % CORES)
+                to = lax.rem(y + dy, ny) * CORES + k
+                for i, (side, at_y, at_k) in enumerate(((0, dy, k), up_row, down_row, (1, dy, k), (-1, dy, k))):
+                    words, e = groups[2 * place[side, at_y] + at_k]
+                    sets[to, i * quarter:(i + 1) * quarter] = words
+                    sets[to, 5 * quarter + i:5 * quarter + i + 1] = e
+            if dy:
+                for dk in range(CORES):
+                    to = row_at(dy, dk)
+                    send(4, sets.at[to], row2.at[r], (to, c))
+            else:
+                to = row_at(0, 1)
+                send(4, sets.at[to], row2.at[r], (to, c))
     row2[r] = sets[r]
-    arrived(6, row2, nrow - 1)
+    arrived(4, row2, nrow - 1)
     picks = []
     for k in range(5):
         tops, bots = [], []
@@ -450,12 +452,11 @@
     inner = matmul(picked, wide_hi[...], NN) + matmul(picked, wide_lo[...], NN)
     out_ref[...] = out_ref[...] + inner[:rhs] + inner[rhs:]
 
-    for phase, buf in ((0, col1), (4, col2)):
-        drained(phase, buf, near * NX - 1)
-        drained(phase + 1, buf, (nz - near) * NX)
-    drained(2, row1, nrow - 1)
-    drained(3, received, ncol - 1)
-    drained(6, row2, nrow - 1)
+    drained(0, col1, ncol - 1)
+    drained(1, row1, nrow - 1)
+    drained(2, received, ncol - 1)
+    drained(3, col2, ncol - 1)
+    drained(4, row2, nrow - 1)
     for d in range(4):
         @pl.when(exists[d])
         def _():
@@ -509,8 +510,8 @@
             dma((4,)),
             dma((4,)),
             dma((4,)),
-            dma((7,)),
-            dma((7,)),
+            dma((5,)),
+            dma((5,)),
             pltpu.SemaphoreType.REGULAR((2,)),
         ],
         compiler_params=pltpu.CompilerParams(collective_id=0, has_side_effects=True),

time: 45.4 us -> 44.7 us (0.985)
  Pallas kernels: 44.7 us -> 44 us
    pallas_call x1, Pallas kernels: 44.7 us -> 44 us  [shards(): pl.pallas_call(functools.partial(kernel, nrow, ncol), name='schwarz', out...]
where the time goes in v5:
time: 44.7 us; the launch traced here: 44.6 us
  Pallas kernels  44 us (98%)
  local copies, waits for them, and re-layouts  0.63 us (1%)
    pallas_call x1, Pallas kernels, shards(): pl.pallas_call(functools.partial(kernel, nrow, ncol), name='schwarz', out...  44 us

profile of v5, /device:TPU:1, one launch (start us, length us, event | category | flops | bytes accessed | tf_op | source)
XLA Modules:
  0.0 44.6 jit_solution(553834301376889469)
XLA Ops:
  0.0 44.0 %schwarz.1 = f32[32,512]{1,0:T(8,128)S(1)} custom-call(bf16[32,512]{1,0:T(8,128)(2,1)} %bitcast.7, s32[1,4]{1,0:T(1,128)} %ib_hbm.1, bf16[512,1024]{1,0:T(8,128)(2,1)} %linv_hbm.1, f32[64,1024]{1,0:T(8,128)} %bitcast.5, s32[1,16384]{1,0:T(1,128)} %bitcast.6, f32[2048,512]{1,0:T(8,128)} %coarse_hbm.1), custom_call_target="tpu_custom_call" | custom-call | tf_op jit(solution)/shard_map/schwarz/pallas_call | solution.py:479
  44.0 0.6 %copy.8 = f32[512,32]{0,1:T(8,128)} copy(f32[512,32]{0,1:T(8,128)S(1)} %bitcast.4) | data formatting | bytes 131072

commit v6 on v5

--- a/solution.py
+++ b/solution.py
@@ -92,20 +92,18 @@
     hot_out,
     col1,
     row1,
+    product,
     pieces,
     received,
     col2,
     sets,
     row2,
     lent,
-    wide_hi,
-    wide_lo,
+    wide,
     load_sem,
-    halo_send,
+    sent,
     halo_recv,
-    lend_send,
     lend_recv,
-    bulk_send,
     bulk_recv,
     passed,
 ):
@@ -157,8 +155,9 @@
     def line_z(dz):
         return (r, lax.rem(z + dz, nz) * NX + x)
 
-    across_x = [line_x(dx) for dx in (1, NX - 1, 2)]
-    near_z = [line_z(dz) for dz in (1, nz - 1, 2, nz - 2)]
+    across_x = [line_x(dx) for dx in far_first(NX)]
+    near_z = [line_z(dz) for dz in (2, nz - 2, 1, nz - 1)]
+    greeted = across_x + near_z
     up = jnp.logical_and(x == NX - 1, exists[2])
     down = jnp.logical_and(x == 0, exists[3])
     barrier = pltpu.get_barrier_semaphore()
@@ -176,7 +175,7 @@
 
     for offset in row_offsets:
         signal(barrier, (row_at(*offset), c))
-    for device in across_x + near_z:
+    for device in greeted:
         signal(barrier, device)
     for i in (5, 1, 2):
         loads[i].start()
@@ -202,27 +201,27 @@
     def halo(d):
         return pltpu.make_async_remote_copy(
             src_ref=outgoing.at[d], dst_ref=incoming.at[d],
-            send_sem=halo_send.at[d], recv_sem=halo_recv.at[d],
+            send_sem=sent.at[0], recv_sem=halo_recv.at[d],
             device_id=target[d], device_id_type=MESH)
 
     def lend(d):
         return pltpu.make_async_remote_copy(
             src_ref=basis.at[:, pl.ds(own + d * BLK, BLK)], dst_ref=lent.at[d],
-            send_sem=lend_send.at[d], recv_sem=lend_recv.at[d],
+            send_sem=sent.at[0], recv_sem=lend_recv.at[d],
             device_id=target[opposite[d]], device_id_type=MESH)
 
     def send(phase, src, dst, device):
         pltpu.make_async_remote_copy(
-            src_ref=src, dst_ref=dst, send_sem=bulk_send.at[phase], recv_sem=bulk_recv.at[phase],
+            src_ref=src, dst_ref=dst, send_sem=sent.at[0], recv_sem=bulk_recv.at[phase],
             device_id=device, device_id_type=MESH).start()
 
     def arrived(phase, buf, count):
         some = buf.at[pl.ds(0, count)]
         pltpu.make_async_copy(some, some, bulk_recv.at[phase]).wait()
 
-    def drained(phase, buf, count):
+    def drained(buf, count):
         some = buf.at[pl.ds(0, count)]
-        pltpu.make_async_copy(some, some, bulk_send.at[phase]).wait()
+        pltpu.make_async_copy(some, some, sent.at[0]).wait()
 
     def spread_col(phase, buf, top, bot, ready):
         largest = jnp.maximum(jnp.abs(top), jnp.abs(bot))
@@ -253,23 +252,23 @@
         return ((jnp.where(low, first, half_roll(second)), jnp.where(low, e, swapped)[:1]),
                 (jnp.where(low, half_roll(first), second), jnp.where(low, swapped, e)[:1]))
 
-    pl.semaphore_wait(barrier, nrow - 1 + len(across_x) + len(near_z) + up.astype(jnp.int32) + down.astype(jnp.int32))
+    pl.semaphore_wait(barrier, nrow - 1 + len(greeted) + up.astype(jnp.int32) + down.astype(jnp.int32))
     for d in range(4):
         @pl.when(exists[d])
         def _():
             halo(d).start()
 
-    for device in across_x + near_z:
+    for device in greeted:
         signal(passed.at[0], device)
     loads[0].wait()
     b_hi, b_lo = split(basis[...])
     basis2[:nev] = b_hi
     basis2[nev:] = b_lo
     partial = matmul(res_ref[...], basis2[:, :own], NT)
-    pl.semaphore_wait(passed.at[0], len(across_x) + len(near_z))
+
+    pl.semaphore_wait(passed.at[0], len(greeted))
     for device in across_x:
         signal(passed.at[1], device)
-
     for d in range(4):
         @pl.when(exists[opposite[d]])
         def _():
@@ -280,13 +279,15 @@
     partial = partial + half_roll(partial)
     spread_col(0, col1, jnp.where(low, partial[:quarter], partial[half:half + quarter]),
                jnp.where(low, partial[quarter:half], partial[half + quarter:]),
-               lambda: pl.semaphore_wait(passed.at[1], len(across_x)))
+               lambda: pl.semaphore_wait(passed.at[1], NX - 1))
 
     span = rows // nz
     loads[1].wait()
     for t in range(nz):
         at = slice(t * span, (t + 1) * span)
-        coarse_t[:width, at], coarse_t[width:, at] = split(coarse[at].T)
+        for h in range(2):
+            turned = split(coarse[at, h * (width // 2):(h + 1) * (width // 2)].T)
+            coarse_t[h * width:h * width + width // 2, at], coarse_t[h * width + width // 2:(h + 1) * width, at] = turned
     loads[2].wait()
     local = jnp.concatenate([res_ref[...], inc], axis=1)
     out_ref[...] = matmul(local, linv[...], NT)
@@ -304,30 +305,36 @@
     lax.fori_loop(0, rows // chunk, build_in, 0)
 
     arrived(0, col1, ncol - 1)
-    part = matmul(gathered(col1), hot_in[...], NN)
-    part = part[:rhs] + part[rhs:]
-    blocks4 = width // LANES
-    for q in range(blocks4):
-        block = part[:, q * LANES:(q + 1) * LANES]
-        e, factor = scale_of(largest_of(block))
-        row1[r, q * half:(q + 1) * half] = to_words(block[:half], block[half:], factor[:1])
-        row1[r, blocks4 * half + q:blocks4 * half + q + 1] = e[:1]
-    for offset in row_offsets:
-        send(1, row1.at[r], row1.at[r], (row_at(*offset), c))
-
-    order = [(0, dy) for dy in range(ny)] + [(side, dy) for dy in far_first(ny) + [0] for side in (1, -1)]
-    place = {key: i for i, key in enumerate(order)}
-    low8 = lane_low((8, LANES))
+    partials = gathered(col1)
+    part_blocks = width // 2 // LANES
+    for h in range(2):
+        part = matmul(partials, hot_in[:, h * (width // 2):(h + 1) * (width // 2)], NN)
+        part = part[:rhs] + part[rhs:]
+        for q in range(part_blocks):
+            block = part[:, q * LANES:(q + 1) * LANES]
+            e, factor = scale_of(largest_of(block))
+            row1[h, r, q * half:(q + 1) * half] = to_words(block[:half], block[half:], factor[:1])
+            row1[h, r, part_blocks * half + q:part_blocks * half + q + 1] = e[:1]
+        for offset in row_offsets:
+            send(1 + h, row1.at[h, r], row1.at[h, r], (row_at(*offset), c))
+
+    def sides(dy):
+        return [((side, dy, 0), (side, dy, 1)) for side in (1, -1)]
+
+    order = [((0, 2, 0), (0, 2, 1)), ((0, 3, 0), (0, 1, 1))] + sides(2)
+    order += [((0, 1, 0), (0, 3, 1)), ((0, 0, 0), (0, 0, 1))] + sides(1) + sides(3) + sides(0)
+    place = {key: 2 * i + j for i, pair in enumerate(order) for j, key in enumerate(pair)}
     wanted = []
-    for side, dy in order:
+    for keys in order:
+        side = keys[0][0]
         safe = jnp.clip(c + side, 0, ncol - 1)
-        first = lax.rem(y + dy, ny) * CORES * ncol + safe
         pair = []
-        for device in (first, first + ncol):
+        for _, dy, k in keys:
+            device = (lax.rem(y + dy, ny) * CORES + k) * ncol + safe
             at = pl.ds(pl.multiple_of((device // 2) * LANES, LANES), LANES)
             pair.append(jnp.broadcast_to(slots_ref[:, at], (8, LANES)))
-        even = jnp.where(low8, pair[0], half_roll(pair[1]))
-        odd = jnp.where(low8, half_roll(pair[0]), pair[1])
+        even = jnp.where(low, pair[0], half_roll(pair[1]))
+        odd = jnp.where(low, half_roll(pair[0]), pair[1])
         both = jnp.where(lax.rem(safe, 2) == 0, even, odd)[:1]
         if side:
             both = jnp.where(exists[2] if side > 0 else exists[3], both, -1)
@@ -342,27 +349,34 @@
 
     lax.fori_loop(0, rows // LANES, build_out, 0)
 
-    arrived(1, row1, nrow - 1)
-    column = []
-    for q in range(blocks4):
-        tops, bots = [], []
-        for i in range(nrow):
-            scale = scale_from(row1[i, blocks4 * half + q:blocks4 * half + q + 1])
-            top, bot = from_words(row1[i, q * half:(q + 1) * half])
-            tops.append(top * scale)
-            bots.append(bot * scale)
-        column.append(jnp.concatenate([tree_sum(tops), tree_sum(bots)], axis=0))
-    column2 = jnp.concatenate(split(jnp.concatenate(column, axis=1)), axis=0)
-    column4 = jnp.concatenate([column2, column2], axis=1)
-
+    def column_half(h):
+        arrived(1 + h, row1.at[h], nrow - 1)
+        column = []
+        for q in range(part_blocks):
+            tops, bots = [], []
+            for i in range(nrow):
+                scale = scale_from(row1[h, i, part_blocks * half + q:part_blocks * half + q + 1])
+                top, bot = from_words(row1[h, i, q * half:(q + 1) * half])
+                tops.append(top * scale)
+                bots.append(bot * scale)
+            column.append(jnp.concatenate([tree_sum(tops), tree_sum(bots)], axis=0))
+        value = jnp.concatenate(split(jnp.concatenate(column, axis=1)), axis=0)
+        return jnp.concatenate([value, value], axis=1)
+
+    first_half = column_half(0)
+    for t in range(nz):
+        at = slice(t * span, (t + 1) * span)
+        part = matmul(first_half, coarse_t[:width, at], NN)
+        product[:, at] = part[:rhs] + part[rhs:]
+    second_half = column_half(1)
     steps = far_first(nz) + [0]
     for batch in (steps[:2], steps[2:5], steps[5:]):
         parts = []
         for dz in batch:
             block = lax.rem(z + dz, nz)
             at = pl.ds(pl.multiple_of(block * span, span), span)
-            part = matmul(column4, coarse_t[:, at], NN)
-            parts.append((block, part[:rhs] + part[rhs:]))
+            part = matmul(second_half, coarse_t[width:, at], NN)
+            parts.append((block, part[:rhs] + part[rhs:] + product[:, at]))
         for block, part in parts:
             for q in range(span // LANES):
                 for i, (words, e) in enumerate(paired_words(part[:, q * LANES:(q + 1) * LANES])):
@@ -371,7 +385,7 @@
         for dz, (block, part) in zip(batch, parts):
             for dx in (2, 1, 3, 0) if dz else (2, 1, 3):
                 to = block * NX + lax.rem(x + dx, NX)
-                send(2, pieces.at[to], received.at[c], (r, to))
+                send(3, pieces.at[to], received.at[c], (r, to))
 
     for d in range(4):
         @pl.when(exists[opposite[d]])
@@ -379,7 +393,7 @@
             lend(d).start()
 
     received[c] = pieces[c]
-    arrived(2, received, ncol - 1)
+    arrived(3, received, ncol - 1)
     tops, bots = [], []
     for i in range(ncol):
         scale = scale_from(received[i, quarter:])
@@ -387,12 +401,12 @@
         tops.append(top * scale)
         bots.append(bot * scale)
     top, bot = tree_sum(tops), tree_sum(bots)
-    spread_col(3, col2, top, bot, lambda: None)
-
-    wide_hi[:nev] = basis2[:nev, :own]
-    wide_lo[:nev] = basis2[nev:, :own]
-    wide_hi[5 * nev:] = jnp.zeros_like(wide_hi[5 * nev:])
-    wide_lo[5 * nev:] = jnp.zeros_like(wide_lo[5 * nev:])
+    spread_col(4, col2, top, bot, lambda: None)
+
+    wide[:nev] = basis2[:nev, :own]
+    wide[6 * nev:7 * nev] = basis2[nev:, :own]
+    for at in (5 * nev, 11 * nev):
+        wide[at:at + nev] = jnp.zeros_like(wide[at:at + nev])
     for d in range(4):
         @pl.when(exists[d])
         def _():
@@ -401,14 +415,14 @@
         l_hi, l_lo = split(lent[d])
         for b in range(own // BLK):
             here = ib_ref[0, d] == b
-            at = slice((d + 1) * nev, (d + 2) * nev), slice(b * BLK, (b + 1) * BLK)
-            wide_hi[at] = jnp.where(here, l_hi, jnp.zeros_like(l_hi))
-            wide_lo[at] = jnp.where(here, l_lo, jnp.zeros_like(l_lo))
-
-    arrived(3, col2, ncol - 1)
+            at = slice(b * BLK, (b + 1) * BLK)
+            wide[(d + 1) * nev:(d + 2) * nev, at] = jnp.where(here, l_hi, jnp.zeros_like(l_hi))
+            wide[(d + 7) * nev:(d + 8) * nev, at] = jnp.where(here, l_lo, jnp.zeros_like(l_lo))
+
+    arrived(4, col2, ncol - 1)
     solution = gathered(col2)
     groups = []
-    for dys, stop in (((2,), ny + 2), ((1, 3), ny + 6), ((0,), ny + 8)):
+    for dys, stop in (((2,), 4), ((1, 3), 10), ((0,), 12)):
         start = len(groups) // 2
         part = matmul(solution, hot_out[:, start * LANES:stop * LANES], NN)
         part = part[:rhs] + part[rhs:]
@@ -420,18 +434,18 @@
                 down_row = (0, (dy + (k - 1) // CORES) % ny, (k - 1) % CORES)
                 to = lax.rem(y + dy, ny) * CORES + k
                 for i, (side, at_y, at_k) in enumerate(((0, dy, k), up_row, down_row, (1, dy, k), (-1, dy, k))):
-                    words, e = groups[2 * place[side, at_y] + at_k]
+                    words, e = groups[place[side, at_y, at_k]]
                     sets[to, i * quarter:(i + 1) * quarter] = words
                     sets[to, 5 * quarter + i:5 * quarter + i + 1] = e
             if dy:
                 for dk in range(CORES):
                     to = row_at(dy, dk)
-                    send(4, sets.at[to], row2.at[r], (to, c))
+                    send(5, sets.at[to], row2.at[r], (to, c))
             else:
                 to = row_at(0, 1)
-                send(4, sets.at[to], row2.at[r], (to, c))
+                send(5, sets.at[to], row2.at[r], (to, c))
     row2[r] = sets[r]
-    arrived(4, row2, nrow - 1)
+    arrived(5, row2, nrow - 1)
     picks = []
     for k in range(5):
         tops, bots = [], []
@@ -449,14 +463,15 @@
             [jnp.where(low, a[i], half_roll(b[i])) for i in range(2)]
             + [jnp.where(low, half_roll(a[i]), b[i]) for i in range(2)], axis=0))
     picked = jnp.concatenate(split(jnp.concatenate(columns, axis=1)), axis=0)
-    inner = matmul(picked, wide_hi[...], NN) + matmul(picked, wide_lo[...], NN)
+    inner = matmul(jnp.concatenate([picked, picked], axis=1), wide[...], NN)
     out_ref[...] = out_ref[...] + inner[:rhs] + inner[rhs:]
 
-    drained(0, col1, ncol - 1)
-    drained(1, row1, nrow - 1)
-    drained(2, received, ncol - 1)
-    drained(3, col2, ncol - 1)
-    drained(4, row2, nrow - 1)
+    drained(col1, ncol - 1)
+    drained(row1.at[0], nrow - 1)
+    drained(row1.at[1], nrow - 1)
+    drained(received, ncol - 1)
+    drained(col2, ncol - 1)
+    drained(row2, nrow - 1)
     for d in range(4):
         @pl.when(exists[d])
         def _():
@@ -496,22 +511,20 @@
             pltpu.VMEM((rows, width), BF16),
             pltpu.VMEM((rows, 3 * width), BF16),
             pltpu.VMEM((ncol, rhs // 4 + 1, LANES), jnp.int32),
-            pltpu.VMEM((nrow, width // LANES * (rhs // 2 + 1), LANES), jnp.int32),
+            pltpu.VMEM((2, nrow, width // 2 // LANES * (rhs // 2 + 1), LANES), jnp.int32),
+            pltpu.VMEM((rhs, rows), F32),
             pltpu.VMEM((ncol, rhs // 4 + 1, LANES), jnp.int32),
             pltpu.VMEM((ncol, rhs // 4 + 1, LANES), jnp.int32),
             pltpu.VMEM((ncol, rhs // 4 + 1, LANES), jnp.int32),
             pltpu.VMEM((nrow, 5 * (rhs // 4 + 1), LANES), jnp.int32),
             pltpu.VMEM((nrow, 5 * (rhs // 4 + 1), LANES), jnp.int32),
             pltpu.VMEM((4, nev, BLK), F32),
-            pltpu.VMEM((6 * nev, own), BF16),
-            pltpu.VMEM((6 * nev, own), BF16),
+            pltpu.VMEM((12 * nev, own), BF16),
             dma((6,)),
+            dma((1,)),
             dma((4,)),
             dma((4,)),
-            dma((4,)),
-            dma((4,)),
-            dma((5,)),
-            dma((5,)),
+            dma((6,)),
             pltpu.SemaphoreType.REGULAR((2,)),
         ],
         compiler_params=pltpu.CompilerParams(collective_id=0, has_side_effects=True),

time: 44.7 us -> 44.2 us (0.989)
  Pallas kernels: 44 us -> 43.5 us
    pallas_call x1, Pallas kernels: 44 us -> 43.5 us  [shards(): pl.pallas_call(functools.partial(kernel, nrow, ncol), name='schwarz', out...]
where the time goes in v6:
time: 44.2 us; the launch traced here: 44.1 us
  Pallas kernels  43.5 us (98%)
  local copies, waits for them, and re-layouts  0.63 us (1%)
    pallas_call x1, Pallas kernels, shards(): pl.pallas_call(functools.partial(kernel, nrow, ncol), name='schwarz', out...  43.5 us

profile of v6, /device:TPU:1, one launch (start us, length us, event | category | flops | bytes accessed | tf_op | source)
XLA Modules:
  0.0 44.1 jit_solution(12327190207045672814)
XLA Ops:
  0.0 43.5 %schwarz.1 = f32[32,512]{1,0:T(8,128)S(1)} custom-call(bf16[32,512]{1,0:T(8,128)(2,1)} %bitcast.7, s32[1,4]{1,0:T(1,128)} %ib_hbm.1, bf16[512,1024]{1,0:T(8,128)(2,1)} %linv_hbm.1, f32[64,1024]{1,0:T(8,128)} %bitcast.5, s32[1,16384]{1,0:T(1,128)} %bitcast.6, f32[2048,512]{1,0:T(8,128)} %coarse_hbm.1), custom_call_target="tpu_custom_call" | custom-call | tf_op jit(solution)/shard_map/schwarz/pallas_call | solution.py:494
  43.5 0.6 %copy.8 = f32[512,32]{0,1:T(8,128)} copy(f32[512,32]{0,1:T(8,128)S(1)} %bitcast.4) | data formatting | bytes 131072

commit v7 on v6

--- a/solution.py
+++ b/solution.py
@@ -13,7 +13,6 @@
 NX = 4
 CORES = 2
 PEAK = 32760.0
-STEPS = 8.0
 TINY = 1e-30
 NT = (((1,), (1,)), ((), ()))
 NN = (((1,), (0,)), ((), ()))
@@ -50,18 +49,22 @@
 
 def scale_of(largest):
     top = jnp.broadcast_to(jnp.max(largest, axis=0, keepdims=True), largest.shape)
-    e = jnp.ceil(jnp.log2(jnp.maximum(top, TINY)) * STEPS)
-    return e.astype(jnp.int32), jnp.exp2(e * (-1.0 / STEPS)) * PEAK
+    e = jnp.ceil(jnp.log2(jnp.maximum(top, TINY)))
+    return e.astype(jnp.int32), jnp.exp2(-e) * PEAK
 
 
 def scale_from(row):
-    return jnp.exp2(row.astype(F32) * (1.0 / STEPS)) * (1.0 / PEAK)
+    return jnp.exp2(row.astype(F32)) * (1.0 / PEAK)
 
 
 def to_words(top, bot, factor):
     a = jnp.round(top * factor).astype(jnp.int32)
     b = jnp.round(bot * factor).astype(jnp.int32)
-    return (a << 16) | (b & 0xFFFF)
+    return pack(a, b)
+
+
+def pack(top, bot):
+    return (top << 16) | (bot & 0xFFFF)
 
 
 def from_words(w):
@@ -128,6 +131,8 @@
         ((dy, dk) for dy in range(ny) for dk in range(CORES) if (dy, dk) != (0, 0)),
         key=lambda o: -(min(o[0], ny - o[0]) + 0.5 * o[1]))
 
+    origin_first = sorted(range(ncol), key=lambda i: min(i // NX, nz - i // NX) + min(i % NX, NX - i % NX))
+
     def col_at(dz, dx):
         return lax.rem(z + dz, nz) * NX + lax.rem(x + dx, NX)
 
@@ -210,6 +215,12 @@
             send_sem=sent.at[0], recv_sem=lend_recv.at[d],
             device_id=target[opposite[d]], device_id_type=MESH)
 
+    def lend_to(directions):
+        for d in directions:
+            @pl.when(exists[opposite[d]])
+            def _():
+                lend(d).start()
+
     def send(phase, src, dst, device):
         pltpu.make_async_remote_copy(
             src_ref=src, dst_ref=dst, send_sem=sent.at[0], recv_sem=bulk_recv.at[phase],
@@ -223,23 +234,38 @@
         some = buf.at[pl.ds(0, count)]
         pltpu.make_async_copy(some, some, sent.at[0]).wait()
 
-    def spread_col(phase, buf, top, bot, ready):
+    def spread_col(phase, buf, top, bot, ready, last=False):
         largest = jnp.maximum(jnp.abs(top), jnp.abs(bot))
         e, factor = scale_of(jnp.maximum(largest, half_roll(largest)))
         buf[c, :quarter] = to_words(top, bot, factor)
         buf[c, quarter:] = e[:1]
         ready()
-        for offset in col_offsets:
-            send(phase, buf.at[c], buf.at[c], (r, col_at(*offset)))
+        if not last:
+            for offset in col_offsets:
+                send(phase, buf.at[c], buf.at[c], (r, col_at(*offset)))
+        for to in origin_first if last else ():
+            @pl.when(c != to)
+            def _():
+                send(phase, buf.at[c], buf.at[c], (r, to))
 
     def gathered(buf):
         columns = []
         for first in range(0, ncol, 2):
             a, b = buf[first, :quarter], buf[first + 1, :quarter]
-            scale = scale_from(jnp.where(low1, buf[first, quarter:], buf[first + 1, quarter:]))
-            quarters = from_words(jnp.where(low, a, half_roll(b))) + from_words(jnp.where(low, half_roll(a), b))
-            columns.append(jnp.concatenate([v * scale for v in quarters], axis=0))
-        return jnp.concatenate(split(jnp.concatenate(columns, axis=1)), axis=0)
+            words = jnp.where(low, a, half_roll(b)), jnp.where(low, half_roll(a), b)
+            e = jnp.where(low1, buf[first, quarter:], buf[first + 1, quarter:])
+            parts = [v for w in words for v in (w >> 24, (w << 16) >> 24)]
+            parts += [v for w in words for v in ((w >> 16) & 0xFF, w & 0xFF)]
+            parts.append(jnp.broadcast_to(e, (half, LANES)))
+            columns.append(jnp.concatenate(parts, axis=0).astype(F32).astype(BF16))
+        return jnp.concatenate(columns, axis=1)
+
+    def select(codes, hot):
+        part = matmul(codes, hot, NN)
+        return (part[:rhs] * 256.0 + part[rhs:2 * rhs]).astype(jnp.int32), part[2 * rhs:2 * rhs + quarter].astype(jnp.int32)
+
+    def halves(first, second):
+        return jnp.where(low, first, half_roll(second)), jnp.where(low, half_roll(first), second)
 
     def largest_of(part):
         return functools.reduce(jnp.maximum, [jnp.abs(part[i:i + quarter]) for i in range(0, rhs, quarter)])
@@ -248,9 +274,7 @@
         e, factor = scale_of(largest_of(part))
         first = to_words(part[:quarter], part[quarter:half], factor)
         second = to_words(part[half:half + quarter], part[half + quarter:], factor)
-        swapped = half_roll(e)
-        return ((jnp.where(low, first, half_roll(second)), jnp.where(low, e, swapped)[:1]),
-                (jnp.where(low, half_roll(first), second), jnp.where(low, swapped, e)[:1]))
+        return list(zip(halves(first, second), (v[:1] for v in halves(e, e))))
 
     pl.semaphore_wait(barrier, nrow - 1 + len(greeted) + up.astype(jnp.int32) + down.astype(jnp.int32))
     for d in range(4):
@@ -308,29 +332,29 @@
     partials = gathered(col1)
     part_blocks = width // 2 // LANES
     for h in range(2):
-        part = matmul(partials, hot_in[:, h * (width // 2):(h + 1) * (width // 2)], NN)
-        part = part[:rhs] + part[rhs:]
+        codes, e = select(partials, hot_in[:, h * (width // 2):(h + 1) * (width // 2)])
         for q in range(part_blocks):
-            block = part[:, q * LANES:(q + 1) * LANES]
-            e, factor = scale_of(largest_of(block))
-            row1[h, r, q * half:(q + 1) * half] = to_words(block[:half], block[half:], factor[:1])
-            row1[h, r, part_blocks * half + q:part_blocks * half + q + 1] = e[:1]
+            at = slice(q * LANES, (q + 1) * LANES)
+            row1[h, r, q * half:(q + 1) * half] = pack(codes[:half, at], codes[half:, at])
+            row1[h, r, part_blocks * half + q:part_blocks * half + q + 1] = e[:1, at]
         for offset in row_offsets:
             send(1 + h, row1.at[h, r], row1.at[h, r], (row_at(*offset), c))
 
-    def sides(dy):
-        return [((side, dy, 0), (side, dy, 1)) for side in (1, -1)]
-
-    order = [((0, 2, 0), (0, 2, 1)), ((0, 3, 0), (0, 1, 1))] + sides(2)
-    order += [((0, 1, 0), (0, 3, 1)), ((0, 0, 0), (0, 0, 1))] + sides(1) + sides(3) + sides(0)
+    lend_to((2, 3))
+
+    def sides(at):
+        return [((side, at, 0), (side, at, 1)) for side in (1, -1)]
+
+    order = [((0, 0, 0), (0, 0, 1)), ((0, 1, 0), (0, 3, 1))] + sides(0)
+    order += [((0, 1, 1), (0, 3, 0)), ((0, 2, 0), (0, 2, 1))] + sides(1) + sides(3) + sides(2)
     place = {key: 2 * i + j for i, pair in enumerate(order) for j, key in enumerate(pair)}
     wanted = []
     for keys in order:
         side = keys[0][0]
         safe = jnp.clip(c + side, 0, ncol - 1)
         pair = []
-        for _, dy, k in keys:
-            device = (lax.rem(y + dy, ny) * CORES + k) * ncol + safe
+        for _, chip, k in keys:
+            device = (chip * CORES + k) * ncol + safe
             at = pl.ds(pl.multiple_of((device // 2) * LANES, LANES), LANES)
             pair.append(jnp.broadcast_to(slots_ref[:, at], (8, LANES)))
         even = jnp.where(low, pair[0], half_roll(pair[1]))
@@ -353,13 +377,10 @@
         arrived(1 + h, row1.at[h], nrow - 1)
         column = []
         for q in range(part_blocks):
-            tops, bots = [], []
-            for i in range(nrow):
-                scale = scale_from(row1[h, i, part_blocks * half + q:part_blocks * half + q + 1])
-                top, bot = from_words(row1[h, i, q * half:(q + 1) * half])
-                tops.append(top * scale)
-                bots.append(bot * scale)
-            column.append(jnp.concatenate([tree_sum(tops), tree_sum(bots)], axis=0))
+            words = tree_sum([row1[h, i, q * half:(q + 1) * half] for i in range(nrow)])
+            at = part_blocks * half + q
+            scale = scale_from(tree_sum([row1[h, i, at:at + 1] for i in range(nrow)]))
+            column.append(jnp.concatenate([v * scale for v in from_words(words)], axis=0))
         value = jnp.concatenate(split(jnp.concatenate(column, axis=1)), axis=0)
         return jnp.concatenate([value, value], axis=1)
 
@@ -387,11 +408,7 @@
                 to = block * NX + lax.rem(x + dx, NX)
                 send(3, pieces.at[to], received.at[c], (r, to))
 
-    for d in range(4):
-        @pl.when(exists[opposite[d]])
-        def _():
-            lend(d).start()
-
+    lend_to((0, 1))
     received[c] = pieces[c]
     arrived(3, received, ncol - 1)
     tops, bots = [], []
@@ -401,7 +418,7 @@
         tops.append(top * scale)
         bots.append(bot * scale)
     top, bot = tree_sum(tops), tree_sum(bots)
-    spread_col(4, col2, top, bot, lambda: None)
+    spread_col(4, col2, top, bot, lambda: None, True)
 
     wide[:nev] = basis2[:nev, :own]
     wide[6 * nev:7 * nev] = basis2[nev:, :own]
@@ -422,40 +439,36 @@
     arrived(4, col2, ncol - 1)
     solution = gathered(col2)
     groups = []
-    for dys, stop in (((2,), 4), ((1, 3), 10), ((0,), 12)):
+    for chips, stop in (((0,), 4), ((1, 3), 10), ((2,), 12)):
         start = len(groups) // 2
-        part = matmul(solution, hot_out[:, start * LANES:stop * LANES], NN)
-        part = part[:rhs] + part[rhs:]
+        codes, e = select(solution, hot_out[:, start * LANES:stop * LANES])
         for q in range(stop - start):
-            groups.extend(paired_words(part[:, q * LANES:(q + 1) * LANES]))
-        for dy in dys:
+            at = slice(q * LANES, (q + 1) * LANES)
+            words = halves(pack(codes[:quarter, at], codes[quarter:half, at]),
+                           pack(codes[half:half + quarter, at], codes[half + quarter:, at]))
+            groups.extend(zip(words, (v[:1] for v in halves(e[:, at], e[:, at]))))
+        for chip in chips:
             for k in range(CORES):
-                up_row = (0, (dy + (k + 1) // CORES) % ny, (k + 1) % CORES)
-                down_row = (0, (dy + (k - 1) // CORES) % ny, (k - 1) % CORES)
-                to = lax.rem(y + dy, ny) * CORES + k
-                for i, (side, at_y, at_k) in enumerate(((0, dy, k), up_row, down_row, (1, dy, k), (-1, dy, k))):
-                    words, e = groups[place[side, at_y, at_k]]
+                to = chip * CORES + k
+                up_row = (0, *divmod((to + 1) % nrow, CORES))
+                down_row = (0, *divmod((to - 1) % nrow, CORES))
+                for i, key in enumerate(((0, chip, k), up_row, down_row, (1, chip, k), (-1, chip, k))):
+                    words, e = groups[place[key]]
                     sets[to, i * quarter:(i + 1) * quarter] = words
                     sets[to, 5 * quarter + i:5 * quarter + i + 1] = e
-            if dy:
-                for dk in range(CORES):
-                    to = row_at(dy, dk)
+
+                @pl.when(r != to)
+                def _():
                     send(5, sets.at[to], row2.at[r], (to, c))
-            else:
-                to = row_at(0, 1)
-                send(5, sets.at[to], row2.at[r], (to, c))
     row2[r] = sets[r]
     arrived(5, row2, nrow - 1)
     picks = []
     for k in range(5):
-        tops, bots = [], []
-        for i in range(nrow):
-            scale = scale_from(row2[i, 5 * quarter + k:5 * quarter + k + 1])
-            top, bot = from_words(row2[i, k * quarter:(k + 1) * quarter])
-            tops.append(top * scale)
-            bots.append(bot * scale)
-        picks.append((tree_sum(tops), tree_sum(bots)))
-    picks.append((jnp.zeros_like(picks[0][0]),) * 2)
+        words = tree_sum([row2[i, k * quarter:(k + 1) * quarter] for i in range(nrow)])
+        at = 5 * quarter + k
+        scale = scale_from(tree_sum([row2[i, at:at + 1] for i in range(nrow)]))
+        picks.append([v * scale for v in from_words(words)])
+    picks.append([jnp.zeros_like(picks[0][0])] * 2)
     columns = []
     for p in range(3):
         a, b = picks[2 * p], picks[2 * p + 1]

time: 44.2 us -> 43.4 us (0.982)
  Pallas kernels: 43.5 us -> 42.7 us
    pallas_call x1, Pallas kernels: 43.5 us -> 42.7 us  [shards(): pl.pallas_call(functools.partial(kernel, nrow, ncol), name='schwarz', out...]
where the time goes in v7:
time: 43.4 us; the launch traced here: 43.3 us
  Pallas kernels  42.7 us (98%)
  local copies, waits for them, and re-layouts  0.63 us (1%)
    pallas_call x1, Pallas kernels, shards(): pl.pallas_call(functools.partial(kernel, nrow, ncol), name='schwarz', out...  42.7 us

profile of v7, /device:TPU:1, one launch (start us, length us, event | category | flops | bytes accessed | tf_op | source)
XLA Modules:
  0.0 43.3 jit_solution(6522096388439796272)
XLA Ops:
  0.0 42.7 %schwarz.1 = f32[32,512]{1,0:T(8,128)S(1)} custom-call(bf16[32,512]{1,0:T(8,128)(2,1)} %bitcast.7, s32[1,4]{1,0:T(1,128)} %ib_hbm.1, bf16[512,1024]{1,0:T(8,128)(2,1)} %linv_hbm.1, f32[64,1024]{1,0:T(8,128)} %bitcast.5, s32[1,16384]{1,0:T(1,128)} %bitcast.6, f32[2048,512]{1,0:T(8,128)} %coarse_hbm.1), custom_call_target="tpu_custom_call" | custom-call | tf_op jit(solution)/shard_map/schwarz/pallas_call | solution.py:507
  42.7 0.6 %copy.8 = f32[512,32]{0,1:T(8,128)} copy(f32[512,32]{0,1:T(8,128)S(1)} %bitcast.4) | data formatting | bytes 131072

commit v8 on v7

--- a/solution.py
+++ b/solution.py
@@ -131,6 +131,7 @@
         ((dy, dk) for dy in range(ny) for dk in range(CORES) if (dy, dk) != (0, 0)),
         key=lambda o: -(min(o[0], ny - o[0]) + 0.5 * o[1]))
 
+    rows_far_first = sorted(range(nrow), key=lambda i: (-min(i // CORES, ny - i // CORES), i % CORES))
     origin_first = sorted(range(ncol), key=lambda i: min(i // NX, nz - i // NX) + min(i % NX, NX - i % NX))
 
     def col_at(dz, dx):
@@ -337,8 +338,11 @@
             at = slice(q * LANES, (q + 1) * LANES)
             row1[h, r, q * half:(q + 1) * half] = pack(codes[:half, at], codes[half:, at])
             row1[h, r, part_blocks * half + q:part_blocks * half + q + 1] = e[:1, at]
-        for offset in row_offsets:
-            send(1 + h, row1.at[h, r], row1.at[h, r], (row_at(*offset), c))
+        for to in rows_far_first:
+            @pl.when(r != to)
+            def _():
+                send(1 + h, row1.at[h, r], row1.at[h, r], (to, c))
+
 
     lend_to((2, 3))
 
@@ -448,7 +452,7 @@
                            pack(codes[half:half + quarter, at], codes[half + quarter:, at]))
             groups.extend(zip(words, (v[:1] for v in halves(e[:, at], e[:, at]))))
         for chip in chips:
-            for k in range(CORES):
+            for k in reversed(range(CORES)):
                 to = chip * CORES + k
                 up_row = (0, *divmod((to + 1) % nrow, CORES))
                 down_row = (0, *divmod((to - 1) % nrow, CORES))

time: 43.4 us -> 43.2 us (level)
  no operation moved by 1% of the time
where the time goes in v8:
time: 43.2 us
  Pallas kernels  42.5 us (98%)
  local copies, waits for them, and re-layouts  0.63 us (1%)
    pallas_call x1, Pallas kernels, shards(): pl.pallas_call(functools.partial(kernel, nrow, ncol), name='schwarz', out...  42.5 us

profile of v8, /device:TPU:1, one launch (start us, length us, event | category | flops | bytes accessed | tf_op | source)
XLA Modules:
  0.0 43.2 jit_solution(2361783998593250406)
XLA Ops:
  0.0 42.5 %schwarz.1 = f32[32,512]{1,0:T(8,128)S(1)} custom-call(bf16[32,512]{1,0:T(8,128)(2,1)} %bitcast.7, s32[1,4]{1,0:T(1,128)} %ib_hbm.1, bf16[512,1024]{1,0:T(8,128)(2,1)} %linv_hbm.1, f32[64,1024]{1,0:T(8,128)} %bitcast.5, s32[1,16384]{1,0:T(1,128)} %bitcast.6, f32[2048,512]{1,0:T(8,128)} %coarse_hbm.1), custom_call_target="tpu_custom_call" | custom-call | tf_op jit(solution)/shard_map/schwarz/pallas_call | solution.py:511
  42.5 0.6 %copy.8 = f32[512,32]{0,1:T(8,128)} copy(f32[512,32]{0,1:T(8,128)S(1)} %bitcast.4) | data formatting | bytes 131072
